TPU v7x, 512 devices: a whole 4x8x8 slice. The times are simulated.
512 devices in a mesh: dp: 8 (over z_hi, x), seq: 64 (over z_lo, y, core).
Axes of the slice: x: 4, y: 8, z: 8 (z_hi: 2, z_lo: 4; z = z_hi * 4 + z_lo), core: 2. Of those that a mesh axis runs over, the one named last changes fastest.
Arguments:
- queries: bfloat16 [8, 2048, 12288], P('dp', None, 'seq'), may hold values from -360 to 360
- latent: bfloat16 [8, 2048, 576], P('dp', 'seq'), may hold values from -6 to 6
- latent_gain: float32 [512], replicated, may hold values from 0.1 to 1.9
- segments: int32 [8, 2048], P('dp', 'seq'), may hold values from 0 to 7, never falling along the last dimension, each value on 1 to 512 neighbouring positions
- up_weight: bfloat16 [512, 16384], P('dp', 'seq'), may hold values from -0.25 to 0.25
- out_grad: bfloat16 [8, 2048, 8192], P('dp', None, 'seq'), may hold values from -6 to 6
- hess_old: float32 [512, 16384], P('dp', 'seq'), may hold values from 0.01 to 0.3
Outputs:
- attn_out: bfloat16 [8, 2048, 8192], P('dp', None, 'seq')
- hess_new: float32 [512, 16384], P('dp', 'seq')
All inputs are finite; a program needn't handle non-finite values.
Results may differ from a plain program's by a relative error of at most 0.0075.
Values may be sent and summed in bfloat16 or wider, within the bound.
No kernel may reach another device: no remote copies, remote signals or barrier semaphores. Data moves between devices by JAX's collectives and lax.ppermute only.
A program may use at most 64 MiB of HBM per device.

v0:
```python
import jax
import jax.numpy as jnp
from jax import lax
from jax.sharding import Mesh
from jax.sharding import PartitionSpec as P

D_LAT = 512
D_ROPE = 64
D_NOPE = 128
D_VAL = 128
SEQ = ("seq_0", "seq_1", "seq_2")


epsilon = 1e-06
ema_decay = 0.99
rope_base = 10000.0
masked_score = -1e30


def copy_for_each(x, axis):
    size = lax.axis_size(axis)
    return lax.all_to_all(jnp.broadcast_to(x[None], (size, *x.shape)), axis, 0, 0, tiled=True)


def in_order(parts, dim):
    parts = jnp.moveaxis(parts, 0, dim)
    shape = parts.shape
    return parts.reshape(*shape[:dim], shape[dim] * shape[dim + 1], *shape[dim + 2 :])


def gathered_by_axis(x, axes, dim):
    far, near = axes
    first = copy_for_each(x, far)
    parts = jnp.swapaxes(copy_for_each(first, near), 0, 1)
    return in_order(parts.reshape(-1, *x.shape), dim)


def sent_together(arrays, axis, dim, along):
    ends, at = ([], 0)
    for a in arrays[:-1]:
        at += a.shape[along]
        ends.append(at)
    both = jnp.concatenate(arrays, axis=along)
    return tuple(jnp.split(gathered_by_axis(both, axis, dim), ends, axis=along))


def collect(x, axis, dim):
    parts = copy_for_each(x, axis)
    return in_order(parts, dim)


def cut_along(x, dim, size):
    shape = x.shape
    parts = x.reshape(*shape[:dim], size, shape[dim] // size, *shape[dim + 1 :])
    return jnp.moveaxis(parts, dim, 0)


def sent_and_summed(x, axis, dim):
    size = lax.axis_size(axis)
    parts = lax.all_to_all(cut_along(x, dim, size), axis, 0, 0, tiled=True)
    return jnp.sum(parts, axis=0)


def doc_positions(seg_ids):
    length = seg_ids.shape[0]
    places = jnp.arange(length, dtype=jnp.int32)
    starts_here = jnp.concatenate([jnp.ones((1,), dtype=bool), seg_ids[1:] != seg_ids[:-1]])
    starts = lax.cummax(jnp.where(starts_here, places, jnp.zeros_like(places)), axis=0)
    return places - starts


def rotate_pairs(values_in, positions):
    half_width = values_in.shape[-1] // 2
    steps_up = jnp.arange(half_width, dtype=jnp.float32)
    frequency = rope_base ** (-(2.0 * steps_up) / values_in.shape[-1])
    angles = positions.astype(jnp.float32)[:, None] * frequency[None, :]
    cosine = jnp.cos(angles)
    sine_term = jnp.sin(angles)
    first_half = values_in[:, :half_width]
    second = values_in[:, half_width:]
    return jnp.concatenate(
        [first_half * cosine - second * sine_term, second * cosine + first_half * sine_term], axis=1
    )


def normalize(latent_rows, latent_gain):
    compressed = latent_rows[:, :D_LAT].astype(jnp.float32)
    spread = jnp.mean(compressed * compressed, axis=-1, keepdims=True)
    return (compressed * lax.rsqrt(spread + epsilon) * latent_gain).astype(jnp.bfloat16)


def project_head(normed_seq, weight_head):
    key_nope = jnp.dot(
        normed_seq, weight_head[:, :D_NOPE], preferred_element_type=jnp.float32
    ).astype(jnp.bfloat16)
    value_rows = jnp.dot(
        normed_seq, weight_head[:, D_NOPE:], preferred_element_type=jnp.float32
    ).astype(jnp.bfloat16)
    return (key_nope, value_rows)


def block_allowed(places, seg_ids, first, lower, upper):
    causal = places[None, first:upper] <= places[lower:upper, None]
    same_doc = seg_ids[None, first:upper] == seg_ids[lower:upper, None]
    return causal & same_doc


def local(queries, latent, latent_gain, segments, up_weight, out_grad, hess_old):
    rope_raw = latent[:, :, D_LAT:]
    normed = normalize(latent[0], latent_gain)[None]
    gathered, rope_all, seg_all = (
        *sent_together((normed, rope_raw), (("seq_0", "seq_1"), "seq_2"), 1, 2),
        gathered_by_axis(segments, (("seq_0", "seq_1"), "seq_2"), 1),
    )
    weight_full = collect(up_weight, "dp", 0)
    seg_ids = seg_all[0]
    positions = doc_positions(seg_ids)
    normed_seq = gathered[0]
    key_rope = rotate_pairs(rope_all[0].astype(jnp.float32), positions).astype(jnp.bfloat16)
    length = seg_ids.shape[0]
    doc_reach = length // 4
    block_rows = min(512, length)
    count_blocks = length // block_rows
    firsts = [
        max(0, index * block_rows - (doc_reach - 1)) // 128 * 128 for index in range(count_blocks)
    ]
    places = jnp.arange(length, dtype=jnp.int32)
    score_scale = (D_NOPE + D_ROPE) ** (-0.5)
    query_rows = queries[0]
    grad_rows_in = out_grad[0]
    q_nope = query_rows[:, :D_NOPE]
    q_rope = rotate_pairs(query_rows[:, D_NOPE:].astype(jnp.float32), positions).astype(
        jnp.bfloat16
    )
    q_full = jnp.concatenate([q_nope, q_rope], axis=1)
    key_nope, value_rows = project_head(normed_seq, weight_full)
    key_full = jnp.concatenate([key_nope, key_rope], axis=1)
    pieces = []
    norm_pieces = []
    for query_block in range(count_blocks):
        lower = query_block * block_rows
        upper = lower + block_rows
        first = firsts[query_block]
        allowed = block_allowed(places, seg_ids, first, lower, upper)
        scores = (
            jnp.dot(
                q_full[lower:upper], key_full[first:upper].T, preferred_element_type=jnp.float32
            )
            * score_scale
        )
        scores = jnp.where(allowed, scores, masked_score)
        row_max = jnp.max(scores, axis=1, keepdims=True)
        expo_rows = jnp.where(allowed, jnp.exp(scores - row_max), 0.0)
        row_sum = jnp.sum(expo_rows, axis=1, keepdims=True)
        prob_low = (expo_rows / row_sum).astype(jnp.bfloat16)
        pieces.append(
            jnp.dot(prob_low, value_rows[first:upper], preferred_element_type=jnp.float32)
        )
        norm_pieces.append(row_max + jnp.log(row_sum))
    output = jnp.concatenate(pieces, axis=0)
    log_norm = jnp.concatenate(norm_pieces, axis=0)
    outputs = output.astype(jnp.bfloat16)
    key_again, value_back = project_head(normed_seq, weight_full)
    key_back = jnp.concatenate([key_again, key_rope], axis=1)
    delta_rows = jnp.sum(grad_rows_in.astype(jnp.float32) * output, axis=1, keepdims=True)
    value_grad = jnp.zeros((length, D_VAL), jnp.float32)
    key_grad = jnp.zeros((length, D_NOPE), jnp.float32)
    for query_block in range(count_blocks):
        lower = query_block * block_rows
        upper = lower + block_rows
        first = firsts[query_block]
        allowed = block_allowed(places, seg_ids, first, lower, upper)
        scores = (
            jnp.dot(
                q_full[lower:upper], key_back[first:upper].T, preferred_element_type=jnp.float32
            )
            * score_scale
        )
        scores = jnp.where(allowed, scores, masked_score)
        prob_rows = jnp.where(allowed, jnp.exp(scores - log_norm[lower:upper]), 0.0)
        prob_low = prob_rows.astype(jnp.bfloat16)
        grad_block = grad_rows_in[lower:upper]
        value_grad = value_grad.at[first:upper].add(
            jnp.dot(prob_low.T, grad_block, preferred_element_type=jnp.float32)
        )
        prob_grad = jnp.dot(
            grad_block, value_back[first:upper].T, preferred_element_type=jnp.float32
        )
        score_grad = (prob_rows * (prob_grad - delta_rows[lower:upper])).astype(jnp.bfloat16)
        key_grad = key_grad.at[first:upper].add(
            jnp.dot(score_grad.T, q_nope[lower:upper], preferred_element_type=jnp.float32)
        )
    key_low = (key_grad * score_scale).astype(jnp.bfloat16)
    value_low = value_grad.astype(jnp.bfloat16)
    columns = jnp.concatenate([key_low, value_low], axis=1)
    attn_out = outputs[None]
    grad_local = jnp.dot(normed_seq.T, columns, preferred_element_type=jnp.float32)
    grad_rows = sent_and_summed(grad_local, "dp", 0)
    hess_new = ema_decay * hess_old + (1.0 - ema_decay) * grad_rows * grad_rows
    return (attn_out, hess_new)


def solution(mesh):
    finer = Mesh(mesh.devices.reshape(mesh.shape["dp"], 4, 8, 2), ("dp", "seq_0", "seq_1", "seq_2"))
    placed = (
        P("dp", None, SEQ),
        P("dp", SEQ, None),
        P(),
        P("dp", SEQ),
        P("dp", SEQ),
        P("dp", None, SEQ),
        P("dp", SEQ),
    )
    return jax.shard_map(
        local,
        mesh=finer,
        in_specs=placed,
        out_specs=(P("dp", None, SEQ), P("dp", SEQ)),
        check_vma=False,
    )
```

profile of v0, /device:TPU:88, one launch (start us, length us, event | category | flops | bytes accessed | tf_op | source)
XLA Modules:
  0.0 163.2 jit_solution(17527344167786425756)
XLA Ops:
  0.6 1.3 broadcast_in_dim.49
  1.9 12.0 %all-to-all-start = ((s32[32,1,32]{2,1,0:T(1,128)}), s32[32,1,32]{2,1,0:T(1,128)S(1)}, u32[]{:S(2)}, u32[]{:S(2)}) async-start(s32[32,1,32]{2,1,0:T(1,128)} %broadcast_in_dim.49), calls=%async_computation | async-start | bytes 32768 | tf_op jit(solution)/shard_map/all_to_all | solution.py:22
  16.4 3.8 %all-to-all-done = s32[32,1,32]{2,1,0:T(1,128)S(1)} async-done(((s32[32,1,32]{2,1,0:T(1,128)}), s32[32,1,32]{2,1,0:T(1,128)S(1)}, u32[]{:S(2)}, u32[]{:S(2)}) %all-to-all-start) | async-done | bytes 4128 | tf_op jit(solution)/shard_map/all_to_all | solution.py:22
  20.2 3.7 %all_to_all.30 = s32[2,1,1024]{2,1,0:T(1,128)S(1)} all-to-all(s32[2,1,1024]{2,1,0:T(1,128)S(1)} %reshape.406), channel_id=1, replica_groups=mesh['dp'=8,'seq_0'=4,'seq_1'=8,'seq_2'=2] {'seq_2'}, dimensions={0} | all-to-all | bytes 16384 | tf_op jit(solution)/shard_map/all_to_all | solution.py:22
  25.1 7.7 %all-to-all-start.2 = ((bf16[32,1,32,576]{3,2,1,0:T(8,128)(2,1)}), bf16[32,1,32,576]{3,2,1,0:T(8,128)(2,1)S(1)}, u32[]{:S(2)}, u32[]{:S(2)}) async-start(bf16[32,1,32,576]{3,2,1,0:T(8,128)(2,1)} %broadcast_in_dim.55), calls=%async_computation.2 | async-start | bytes 2621440 | tf_op jit(solution)/shard_map/all_to_all | solution.py:22
  36.1 31.4 %all-to-all-done.2 = bf16[32,1,32,576]{3,2,1,0:T(8,128)(2,1)S(1)} async-done(((bf16[32,1,32,576]{3,2,1,0:T(8,128)(2,1)}), bf16[32,1,32,576]{3,2,1,0:T(8,128)(2,1)S(1)}, u32[]{:S(2)}, u32[]{:S(2)}) %all-to-all-start.2) | async-done | bytes 1179680 | tf_op jit(solution)/shard_map/all_to_all | solution.py:22
  67.7 6.8 %all_to_all.31 = bf16[2,32,1,32,576]{4,3,1,2,0:T(8,128)(2,1)} all-to-all(bf16[2,32,1,32,576]{4,3,1,2,0:T(8,128)(2,1)S(1)} %broadcast_in_dim.57), channel_id=1, replica_groups=mesh['dp'=8,'seq_0'=4,'seq_1'=8,'seq_2'=2] {'seq_2'}, dimensions={0} | all-to-all | bytes 4718592 | tf_op jit(solution)/shard_map/all_to_all | solution.py:22
  75.2 10.0 %all-to-all-start.4 = ((bf16[8,64,256]{2,1,0:T(8,128)(2,1)}), bf16[8,64,256]{2,1,0:T(8,128)(2,1)S(1)}, u32[]{:S(2)}, u32[]{:S(2)}) async-start(bf16[8,64,256]{2,1,0:T(8,128)(2,1)} %broadcast_in_dim.58), calls=%async_computation.4 | async-start | bytes 524288 | tf_op jit(solution)/shard_map/all_to_all | solution.py:22
  85.9 2.2 %copy.16 = bf16[32,2,1,32,576]{4,3,1,0,2:T(8,128)(2,1)S(1)} copy(bf16[32,2,1,32,576]{4,3,0,2,1:T(8,128)(2,1)} %bitcast.135) | data formatting | bytes 4718592 | tf_op jit(solution)/shard_map/transpose | solution.py:34
  89.0 10.0 %all-to-all-done.4 = bf16[8,64,256]{2,1,0:T(8,128)(2,1)S(1)} async-done(((bf16[8,64,256]{2,1,0:T(8,128)(2,1)}), bf16[8,64,256]{2,1,0:T(8,128)(2,1)S(1)}, u32[]{:S(2)}, u32[]{:S(2)}) %all-to-all-start.4) | async-done | bytes 262176 | tf_op jit(solution)/shard_map/all_to_all | solution.py:22
  99.0 1.6 convolution_convert_fusion.1
  100.6 1.5 convolution_convert_fusion
  102.1 1.2 copy.34
  103.4 1.4 fusion.77
  115.5 1.5 slice_bitcast_fusion
  118.0 1.2 fusion.57
  119.2 2.8 %fusion.23 = f32[512,128]{0,1:T(8,128)} fusion(f32[512,512]{0,1:T(8,128)} %copy-done.8, f32[512]{0:T(512)S(1)} %get-tuple-element.114, f32[512]{0:T(512)} %copy-done.43, s32[512]{0:T(512)S(1)} %eq.38, s32[512]{0:T(512)S(1)} %iota_add_fusion.6, bf16[2048,192]{0,1:T(8,128)(2,1)} %bitcast.138, bf16[2048,128]{1,0:T(8,128)(2,1)} %convolution_convert_fusion, ...), kind=kOutput, calls=%fused_computation.49 | convolution fusion | flops 136314880 | bytes 1716224 | tf_op jit(solution)/shard_map/dot_general | solution.py:191
  123.1 2.1 %fusion.29 = f32[2048,128]{0,1:T(8,128)S(1)} fusion(f32[2048,128]{0,1:T(8,128)S(1)} %scatter-add.26, f32[512,1024]{1,0:T(8,128)S(1)} %copy-done.2, f32[512]{0:T(512)} %get-tuple-element.113, f32[512]{0:T(512)} %log_add_fusion.2, bf16[2048,128]{1,0:T(8,128)(2,1)} %convolution_convert_fusion, bf16[2048,192]{0,1:T(8,128)(2,1)} %bitcast.139, ...), kind=kOutput, calls=%fused_computation.55 | convolution fusion | flops 272760832 | bytes 3686400 | tf_op jit(solution)/shard_map/dot_general | solution.py:191
  125.2 2.7 %fusion.27 = f32[2048,128]{0,1:T(8,128)S(1)} fusion(f32[2048,128]{0,1:T(8,128)S(1)} %fusion.29, f32[512,1024]{1,0:T(8,128)} %copy-done.3, f32[512]{0:T(512)} %get-tuple-element.112, f32[512]{0:T(512)} %log_add_fusion.1, bf16[2048,128]{1,0:T(8,128)(2,1)} %convolution_convert_fusion, bf16[2048,192]{0,1:T(8,128)(2,1)} %bitcast.140, ...), kind=kOutput, calls=%fused_computation.53 | convolution fusion | flops 272760832 | bytes 3686400 | tf_op jit(solution)/shard_map/dot_general | solution.py:191
  128.0 2.9 %fusion.25 = f32[2048,128]{0,1:T(8,128)S(1)} fusion(f32[2048,128]{0,1:T(8,128)S(1)} %fusion.27, f32[512,1024]{1,0:T(8,128)} %copy-done.5, f32[512]{0:T(512)} %get-tuple-element.111, f32[512]{0:T(512)} %log_add_fusion, bf16[2048,128]{1,0:T(8,128)(2,1)} %convolution_convert_fusion, bf16[2048,192]{0,1:T(8,128)(2,1)} %bitcast.141, ...), kind=kOutput, calls=%fused_computation.51 | convolution fusion | flops 272760832 | bytes 3686400 | tf_op jit(solution)/shard_map/dot_general | solution.py:191
  137.8 2.5 %copy.24 = bf16[512,2048]{1,0:T(8,128)(2,1)} copy(bf16[512,2048]{0,1:T(8,128)(2,1)S(1)} %copy-done) | data formatting | bytes 4194304 | tf_op jit(solution)/shard_map/dot_general | solution.py:197
  140.2 3.2 %fusion.34 = f32[8,64,256]{2,1,0:T(8,128)} fusion(bf16[8,64,2048]{2,1,0:T(8,128)(2,1)} %bitcast.137, bf16[2048,128]{0,1:T(8,128)(2,1)S(1)} %convert_element_type.112, bf16[2048,128]{0,1:T(8,128)(2,1)S(1)} %copy-done.16), kind=kOutput, calls=%fused_computation.59 | convolution fusion | flops 538968064 | bytes 3670016 | tf_op jit(solution)/shard_map/dot_general | solution.py:197
  143.5 3.6 %all-to-all-start.5 = ((f32[8,64,256]{2,1,0:T(8,128)}), f32[8,64,256]{2,1,0:T(8,128)S(1)}, u32[]{:S(2)}, u32[]{:S(2)}) async-start(f32[8,64,256]{2,1,0:T(8,128)} %fusion.34), calls=%async_computation.5 | async-start | bytes 1048576 | tf_op jit(solution)/shard_map/all_to_all | solution.py:60
  148.0 14.4 %all-to-all-done.5 = f32[8,64,256]{2,1,0:T(8,128)S(1)} async-done(((f32[8,64,256]{2,1,0:T(8,128)}), f32[8,64,256]{2,1,0:T(8,128)S(1)}, u32[]{:S(2)}, u32[]{:S(2)}) %all-to-all-start.5) | async-done | bytes 524320 | tf_op jit(solution)/shard_map/all_to_all | solution.py:60
  (174 shorter events, 30.0 us)
Async XLA Ops:
  1.9 18.3 %all-to-all-start = ((s32[32,1,32]{2,1,0:T(1,128)}), s32[32,1,32]{2,1,0:T(1,128)S(1)}, u32[]{:S(2)}, u32[]{:S(2)}) async-start(s32[32,1,32]{2,1,0:T(1,128)} %broadcast_in_dim.49), calls=%async_computation | async-start | bytes 32768 | tf_op jit(solution)/shard_map/all_to_all | solution.py:22
  16.3 16.5 %copy-start.13 = (bf16[1,2048,192]{1,2,0:T(8,128)(2,1)S(1)}, bf16[1,2048,192]{1,2,0:T(8,128)(2,1)}, u32[]{:S(2)}) copy-start(bf16[1,2048,192]{1,2,0:T(8,128)(2,1)} %param.23) | copy-start | bytes 2359300
  25.1 42.3 %all-to-all-start.2 = ((bf16[32,1,32,576]{3,2,1,0:T(8,128)(2,1)}), bf16[32,1,32,576]{3,2,1,0:T(8,128)(2,1)S(1)}, u32[]{:S(2)}, u32[]{:S(2)}) async-start(bf16[32,1,32,576]{3,2,1,0:T(8,128)(2,1)} %broadcast_in_dim.55), calls=%async_computation.2 | async-start | bytes 2621440 | tf_op jit(solution)/shard_map/all_to_all | solution.py:22
  33.7 74.4 %copy-start.38 = (s32[512]{0:T(512)}, s32[512]{0:T(512)S(1)}, u32[]{:S(2)}) copy-start(s32[512]{0:T(512)S(1)} %iota_add_fusion.5) | copy-start | bytes 6148
  33.8 77.3 %copy-start.36 = (s32[512]{0:T(512)}, s32[512]{0:T(512)S(1)}, u32[]{:S(2)}) copy-start(s32[512]{0:T(512)S(1)} %iota_add_fusion.4) | copy-start | bytes 6148
  33.8 80.2 %copy-start.34 = (s32[512]{0:T(512)}, s32[512]{0:T(512)S(1)}, u32[]{:S(2)}) copy-start(s32[512]{0:T(512)S(1)} %iota_add_fusion.3) | copy-start | bytes 6148
  33.8 74.3 %copy-start.26 = (s32[1024]{0:T(1024)}, s32[1024]{0:T(1024)S(1)}, u32[]{:S(2)}) copy-start(s32[1024]{0:T(1024)S(1)} %iota_add_fusion.2) | copy-start | bytes 12292
  33.8 77.2 %copy-start.24 = (s32[1024]{0:T(1024)}, s32[1024]{0:T(1024)S(1)}, u32[]{:S(2)}) copy-start(s32[1024]{0:T(1024)S(1)} %iota_add_fusion.1) | copy-start | bytes 12292
  33.8 80.2 %copy-start.22 = (s32[1024]{0:T(1024)}, s32[1024]{0:T(1024)S(1)}, u32[]{:S(2)}) copy-start(s32[1024]{0:T(1024)S(1)} %iota_add_fusion) | copy-start | bytes 12292
  36.1 72.1 %copy-start.28 = (s32[512]{0:T(512)}, s32[512]{0:T(512)S(1)}, u32[]{:S(2)}) copy-start(s32[512]{0:T(512)S(1)} %eq.44) | copy-start | bytes 6148
  67.7 6.8 %copy-start.19 = (bf16[64,256]{1,0:T(8,128)(2,1)S(1)}, bf16[64,256]{1,0:T(8,128)(2,1)}, u32[]{:S(2)}) copy-start(bf16[64,256]{1,0:T(8,128)(2,1)} %param.27) | copy-start | bytes 98308
  75.2 23.8 %all-to-all-start.4 = ((bf16[8,64,256]{2,1,0:T(8,128)(2,1)}), bf16[8,64,256]{2,1,0:T(8,128)(2,1)S(1)}, u32[]{:S(2)}, u32[]{:S(2)}) async-start(bf16[8,64,256]{2,1,0:T(8,128)(2,1)} %broadcast_in_dim.58), calls=%async_computation.4 | async-start | bytes 524288 | tf_op jit(solution)/shard_map/all_to_all | solution.py:22
  85.4 25.6 %copy-start.30 = (s32[512]{0:T(512)}, s32[512]{0:T(512)S(1)}, u32[]{:S(2)}) copy-start(s32[512]{0:T(512)S(1)} %eq.49) | copy-start | bytes 6148
  85.6 28.4 %copy-start.32 = (s32[512]{0:T(512)}, s32[512]{0:T(512)S(1)}, u32[]{:S(2)}) copy-start(s32[512]{0:T(512)S(1)} %eq.54) | copy-start | bytes 6148
  85.7 28.3 %copy-start.20 = (s32[1024]{0:T(1024)}, s32[1024]{0:T(1024)S(1)}, u32[]{:S(2)}) copy-start(s32[1024]{0:T(1024)S(1)} %eq.52) | copy-start | bytes 12292
  105.4 12.6 %copy-start.8 = (f32[512,512]{0,1:T(8,128)}, f32[512,512]{0,1:T(8,128)S(1)}, u32[]{:S(2)}) copy-start(f32[512,512]{0,1:T(8,128)S(1)} %get-tuple-element.122) | copy-start | bytes 3145732
  106.0 12.0 %copy-start.43 = (f32[512]{0:T(512)}, f32[512]{0:T(512)S(1)}, u32[]{:S(2)}) copy-start(f32[512]{0:T(512)S(1)} %log_add_fusion.3) | copy-start | bytes 6148
  111.9 5.1 %copy-start.9 = (f32[512,128]{1,0:T(8,128)}, f32[512,128]{1,0:T(8,128)S(1)}, u32[]{:S(2)}) copy-start(f32[512,128]{1,0:T(8,128)S(1)} %fusion.53) | copy-start | bytes 786436
  119.2 3.9 %copy-start.2 = (f32[512,1024]{1,0:T(8,128)S(1)}, f32[512,1024]{1,0:T(8,128)}, u32[]{:S(2)}) copy-start(f32[512,1024]{1,0:T(8,128)} %copy-done.1) | copy-start | bytes 6291460
  125.2 2.8 %copy-start.21 = (s32[1024]{0:T(1024)S(1)}, s32[1024]{0:T(1024)}, u32[]{:S(2)}) copy-start(s32[1024]{0:T(1024)} %copy-done.20) | copy-start | bytes 12292
  140.2 6.9 %copy-start.10 = (f32[512,128]{1,0:T(8,128)S(1)}, f32[512,128]{1,0:T(8,128)}, u32[]{:S(2)}) copy-start(f32[512,128]{1,0:T(8,128)} %copy-done.9) | copy-start | bytes 786436
  140.2 6.9 %copy-start.12 = (f32[512,128]{1,0:T(8,128)S(1)}, f32[512,128]{1,0:T(8,128)}, u32[]{:S(2)}) copy-start(f32[512,128]{1,0:T(8,128)} %copy-done.11) | copy-start | bytes 786436
  143.5 19.0 %copy-start.18 = (f32[64,256]{1,0:T(8,128)S(1)}, f32[64,256]{1,0:T(8,128)}, u32[]{:S(2)}) copy-start(f32[64,256]{1,0:T(8,128)} %param.29) | copy-start | bytes 196612
  143.5 19.0 %all-to-all-start.5 = ((f32[8,64,256]{2,1,0:T(8,128)}), f32[8,64,256]{2,1,0:T(8,128)S(1)}, u32[]{:S(2)}, u32[]{:S(2)}) async-start(f32[8,64,256]{2,1,0:T(8,128)} %fusion.34), calls=%async_computation.5 | async-start | bytes 1048576 | tf_op jit(solution)/shard_map/all_to_all | solution.py:60
  (25 other events, 43.5 us)
where the time goes:
time: 164 us; the launch traced here: 163 us
  waiting for transfers between devices  59.6 us (36%)
  starting transfers between devices  33.4 us (20%)
  matrix products  26.2 us (16%)
  local copies, waits for them, and re-layouts  20.2 us (12%)
  other arithmetic  11.8 us (7%)
  blocking collectives  10.5 us (6%)
    all_to_all x3, waiting for transfers between devices, copy_for_each(): lax.all_to_all(jnp.broadcast_to(x[None], (size, *x.shape)), axis, 0, 0, t...  45.2 us
    all_to_all x3, starting transfers between devices, copy_for_each(): lax.all_to_all(jnp.broadcast_to(x[None], (size, *x.shape)), axis, 0, 0, t...  29.8 us
    all_to_all x1, waiting for transfers between devices, sent_and_summed(): parts = lax.all_to_all(cut_along(x, dim, size), axis, 0, 0, tiled=True)  14.4 us
    dot_general x4, matrix products, local(): jnp.dot(score_grad.T, q_nope[lower:upper], preferred_element_type=jnp.flo...  10.6 us
    all_to_all x2, blocking collectives, copy_for_each(): lax.all_to_all(jnp.broadcast_to(x[None], (size, *x.shape)), axis, 0, 0, t...  10.5 us
    unnamed x94, local copies, waits for them, and re-layouts  4.09 us
    dot_general x2, local copies, waits for them, and re-layouts, local(): jnp.dot(normed_seq.T, columns, preferred_element_type=jnp.float32)  3.97 us
    all_to_all x1, starting transfers between devices, sent_and_summed(): parts = lax.all_to_all(cut_along(x, dim, size), axis, 0, 0, tiled=True)  3.62 us
  transfers between devices with their start and end apart: 4, of which 4 were waited for; matrix products, arithmetic and copies ran while one was open for 6% of the time, Pallas kernels for 0%

commit v1 on v0

v1 whole, which is shorter than its diff:
```python
import math

import jax
import jax.numpy as jnp
import numpy as np
from jax import lax
from jax.experimental import pallas as pl
from jax.experimental.pallas import tpu as pltpu
from jax.sharding import Mesh
from jax.sharding import PartitionSpec as P

D_LAT = 512
D_ROPE = 64
D_NOPE = 128
D_VAL = 128
D_ROW = 640
BLOCK = 256
SEQ = ("zl", "y", "c")
DP = ("zh", "x")

epsilon = 1e-06
ema_decay = 0.99
rope_base = 10000.0
masked_score = -1e30
score_scale = (D_NOPE + D_ROPE) ** (-0.5)
f32 = jnp.float32
bf16 = jnp.bfloat16


def shifted(x, axis, step):
    size = lax.axis_size(axis)
    return lax.ppermute(x, axis, [(i, (i + step) % size) for i in range(size)])


def copy_for_each(x, axis):
    size = lax.axis_size(axis)
    return lax.all_to_all(jnp.broadcast_to(x[None], (size, *x.shape)), axis, 0, 0, tiled=True)


def normalize(latent_rows, latent_gain):
    compressed = latent_rows[:, :D_LAT].astype(f32)
    spread = jnp.mean(compressed * compressed, axis=-1, keepdims=True)
    return (compressed * lax.rsqrt(spread + epsilon) * latent_gain).astype(bf16)


def nt(a, b):
    return lax.dot_general(a, b, (((1,), (1,)), ((), ())), preferred_element_type=f32)


def nn(a, b):
    return lax.dot_general(a, b, (((1,), (0,)), ((), ())), preferred_element_type=f32)


def tn(a, b):
    return lax.dot_general(a, b, (((0,), (0,)), ((), ())), preferred_element_type=f32)


Y_OFFSETS = (-3, 0, 3, -4, -1, 2, -2, 1)


def constants():
    half = D_ROPE // 2
    freq = rope_base ** (-(2.0 * np.arange(half)) / D_ROPE)
    freq_row = np.zeros((1, 128), np.float32)
    freq_row[0, :half] = freq
    freq_row[0, half:D_ROPE] = freq
    angles = np.arange(BLOCK)[:, None] * np.concatenate([freq, freq])[None, :]
    table = np.zeros((BLOCK, 256), np.float32)
    table[:, :D_ROPE] = np.cos(angles)
    table[:, 128 : 128 + D_ROPE] = np.sin(angles)
    pick = np.zeros((128, 384), np.float32)
    for i in range(half):
        pick[i, i] = 1.0
        pick[half + i, half + i] = 1.0
        pick[half + i, 128 + i] = -1.0
        pick[i, 128 + half + i] = 1.0
    pick[D_ROPE, 256:] = 1.0
    return freq_row, table, pick


def kernel(
    place, mine, other, queries, grads, weight, freq, table, pick,
    out, gradient,
    lat, hot, key, query, val, val_t, starts, key_grad, val_grad, firsts,
):
    length = lat.shape[0]
    blocks = length // BLOCK
    y, c = place[0], place[1]
    own = mine.shape[0] // (4 * 8)
    for z in range(4):
        for j, away in enumerate(Y_OFFSETS):
            at = (z * 8 + lax.rem(y + (away + 8), 8)) * (2 * own)
            rows = slice((j * 4 + z) * own, (j * 4 + z + 1) * own)
            lat[pl.ds(pl.multiple_of(at + c * own, own), own), :] = mine[rows, :]
            lat[pl.ds(pl.multiple_of(at + (1 - c) * own, own), own), :] = other[rows, :]

    lane = lax.broadcasted_iota(jnp.int32, (BLOCK, 128), 1)
    row = lax.broadcasted_iota(jnp.int32, (BLOCK, 128), 0)
    doc = (lane & 7).astype(f32)
    first = jnp.full((1, 128), 8192, jnp.int32)
    for i in range(blocks):
        at = i * BLOCK
        number = nn(lat[at : at + BLOCK, D_LAT:], pick[:, 256:])
        here = number == doc
        hot[at : at + BLOCK, :] = jnp.where(here, 1.0, 0.0).astype(bf16)
        first = jnp.minimum(
            first, jnp.min(jnp.where(here, row + at, 8192), axis=0, keepdims=True)
        )
    lane8 = lax.broadcasted_iota(jnp.int32, (8, 128), 1)
    row8 = lax.broadcasted_iota(jnp.int32, (8, 128), 0)
    first8 = jnp.broadcast_to(first, (8, 128))
    column = jnp.sum(jnp.where(lane8 == row8, first8, 0).astype(f32), axis=1, keepdims=True)
    low = first8 & 255
    split = jnp.where(lane8 < 8, first8 - low, jnp.where(lane8 < 16, low, 0))
    split = split.astype(f32).astype(bf16)

    @pl.loop(0, blocks)
    def prepare(i):
        at = pl.multiple_of(i * BLOCK, BLOCK)
        rows = pl.ds(at, BLOCK)
        marks = hot[rows, :]
        begun = nt(split, marks)
        starts[:, rows] = begun
        firsts[i] = begun[0, 0].astype(jnp.int32)
        theta = (column - lax.convert_element_type(at, f32)) * freq[...]
        both = jnp.concatenate([jnp.cos(theta), jnp.sin(theta)], axis=1)
        high = both.astype(bf16).astype(f32)
        middle = (both - high).astype(bf16).astype(f32)
        last = both - high - middle
        parts = jnp.concatenate([high, middle, last, jnp.zeros_like(both)], axis=0).astype(bf16)
        turn = nn(marks[:, :32], parts)
        cos_s, sin_s = turn[:, :128], turn[:, 128:]
        cos_b, sin_b = table[:, :128], table[:, 128:]
        cosine = cos_b * cos_s + sin_b * sin_s
        sine = sin_b * cos_s - cos_b * sin_s
        raw = nn(lat[rows, D_LAT:], pick[:, :256])
        key[rows, D_NOPE:] = (raw[:, :128] * cosine + raw[:, 128:] * sine).astype(bf16)
        raw = nn(queries[rows, D_NOPE:], pick[:D_ROPE, :256])
        query[rows, :D_NOPE] = queries[rows, :D_NOPE]
        query[rows, D_NOPE:] = (raw[:, :128] * cosine + raw[:, 128:] * sine).astype(bf16)
        pair = nn(lat[rows, :D_LAT], weight[...])
        key[rows, :D_NOPE] = pair[:, :D_NOPE].astype(bf16)
        val[rows, :] = pair[:, D_NOPE:].astype(bf16)
        val_t[:, rows] = pair[:, D_NOPE:].T.astype(bf16)
        key_grad[rows, :] = jnp.zeros((BLOCK, D_NOPE), f32)
        val_grad[rows, :] = jnp.zeros((BLOCK, D_VAL), f32)

    token = lax.broadcasted_iota(jnp.int32, (BLOCK, BLOCK), 0)
    asker = lax.broadcasted_iota(jnp.int32, (BLOCK, BLOCK), 1)

    def attend(i, count):
        at = pl.multiple_of(i * BLOCK, BLOCK)
        rows = pl.ds(at, BLOCK)
        begun = starts[0:1, rows].astype(jnp.int32)
        q_full = query[rows, :]
        grad = grads[rows, :]
        spans = [pl.ds(pl.multiple_of(at - (count - 1 - j) * BLOCK, BLOCK), BLOCK) for j in range(count)]
        scores = []
        for j, span in enumerate(spans):
            s = nt(key[span, :], q_full) * (score_scale * math.log2(math.e))
            allowed = token >= begun - (at - (count - 1 - j) * BLOCK)
            if j == count - 1:
                allowed = allowed & (token <= asker)
            scores.append(jnp.where(allowed, s, masked_score))
        top = jnp.max(scores[0], axis=0, keepdims=True)
        for s in scores[1:]:
            top = jnp.maximum(top, jnp.max(s, axis=0, keepdims=True))
        expo = [jnp.exp2(s - top) for s in scores]
        total = jnp.sum(expo[0], axis=0, keepdims=True)
        for e in expo[1:]:
            total = total + jnp.sum(e, axis=0, keepdims=True)
        inverse = 1.0 / total
        probs = [e * inverse for e in expo]
        lows = [p.astype(bf16) for p in probs]
        prob_grads = [nt(val[span, :], grad) for span in spans]
        delta = jnp.zeros((1, BLOCK), f32)
        for p, g in zip(lows, prob_grads):
            delta = delta + jnp.sum(p.astype(f32) * g, axis=0, keepdims=True)
        result = jnp.zeros((D_VAL, BLOCK), f32)
        for j, span in enumerate(spans):
            result = result + nn(val_t[:, span], lows[j])
            val_grad[span, :] += nn(lows[j], grad)
            score_grad = (probs[j] * (prob_grads[j] - delta)).astype(bf16)
            key_grad[span, :] += nn(score_grad, q_full[:, :D_NOPE])
        out[rows, :] = result.T.astype(bf16)

    @pl.loop(0, blocks)
    def attention(i):
        at = i * BLOCK
        start = firsts[i]
        count = 1 + (start < at).astype(jnp.int32) + (start < at - BLOCK).astype(jnp.int32)
        for n in (1, 2, 3):

            @pl.when(count == n)
            def _():
                attend(i, n)

    total = jnp.zeros((D_LAT, 256), f32)
    for i in range(blocks):
        rows = slice(i * BLOCK, (i + 1) * BLOCK)
        columns = jnp.concatenate([key_grad[rows, :] * score_scale, val_grad[rows, :]], axis=1)
        total = total + tn(lat[rows, :D_LAT], columns.astype(bf16))
    gradient[...] = total.astype(bf16)


def head(place, mine, other, queries, grads, weight):
    length = queries.shape[0]
    freq, table, pick = constants()
    vmem = pl.BlockSpec(memory_space=pltpu.VMEM)
    return pl.pallas_call(
        kernel,
        out_shape=(
            jax.ShapeDtypeStruct((length, D_VAL), bf16),
            jax.ShapeDtypeStruct((D_LAT, D_NOPE + D_VAL), bf16),
        ),
        in_specs=[pl.BlockSpec(memory_space=pltpu.SMEM)] + [vmem] * 8,
        out_specs=(vmem, vmem),
        scratch_shapes=[
            pltpu.VMEM((length, D_ROW), bf16),
            pltpu.VMEM((length, 128), bf16),
            pltpu.VMEM((length, 256), bf16),
            pltpu.VMEM((length, 256), bf16),
            pltpu.VMEM((length, D_VAL), bf16),
            pltpu.VMEM((D_VAL, length), bf16),
            pltpu.VMEM((8, length), f32),
            pltpu.VMEM((length, D_NOPE), f32),
            pltpu.VMEM((length, D_VAL), f32),
            pltpu.SMEM((length // BLOCK,), jnp.int32),
        ],
        compiler_params=pltpu.CompilerParams(vmem_limit_bytes=48 * 1024 * 1024),
        name="head",
    )(place, mine, other, queries, grads, weight, jnp.asarray(freq), jnp.asarray(table), jnp.asarray(pick, bf16))


def local(queries, latent, latent_gain, segments, up_weight, out_grad, hess_old):
    rows = latent.shape[1]
    normed = normalize(latent[0], latent_gain)
    number = jnp.broadcast_to(segments[0][:, None], (rows, D_ROW - D_LAT - D_ROPE)).astype(bf16)
    mine = jnp.concatenate([normed, latent[0][:, D_LAT:], number], axis=1)

    weight = jnp.stack([up_weight, shifted(up_weight, "zh", 1)])
    line = copy_for_each(mine, "zl").reshape(-1, D_ROW)
    upper = shifted(line, "y", 3)
    lower = shifted(line, "y", -3)
    three = jnp.concatenate([upper, line, lower], axis=0)
    left = shifted(three, "y", 1)
    right = shifted(three[: 2 * line.shape[0]], "y", -1)
    half = jnp.concatenate([three, left, right], axis=0)
    other = shifted(half, "c", 1)
    weight = copy_for_each(weight, "x")
    up = lax.axis_index("zh")
    weight = jnp.where(up == 0, weight, weight[:, ::-1])
    weight = jnp.swapaxes(weight, 0, 1).reshape(D_LAT, D_NOPE + D_VAL)

    place = jnp.stack([lax.axis_index("y"), lax.axis_index("c")]).astype(jnp.int32)
    attn_out, grad = head(place, half, other, queries[0], out_grad[0], weight)

    share = hess_old.shape[0]
    grad = jnp.swapaxes(grad.reshape(2, 4, share, -1), 0, 1)
    parts = lax.all_to_all(grad, "x", 0, 0, tiled=True)
    summed = jnp.sum(parts.astype(f32), axis=0)
    sent = shifted(jnp.where(up == 0, summed[1], summed[0]).astype(bf16), "zh", 1)
    total = jnp.where(up == 0, summed[0], summed[1]) + sent.astype(f32)
    hess_new = ema_decay * hess_old + (1.0 - ema_decay) * total * total
    return (attn_out[None], hess_new)


def solution(mesh):
    finer = Mesh(mesh.devices.reshape(2, 4, 4, 8, 2), ("zh", "x", "zl", "y", "c"))
    placed = (
        P(DP, None, SEQ),
        P(DP, SEQ, None),
        P(),
        P(DP, SEQ),
        P(DP, SEQ),
        P(DP, None, SEQ),
        P(DP, SEQ),
    )
    return jax.shard_map(
        local,
        mesh=finer,
        in_specs=placed,
        out_specs=(P(DP, None, SEQ), P(DP, SEQ)),
        check_vma=False,
    )
```

time: 164 us -> 113 us (0.69)
  the two profiles are of different devices: /device:TPU:88 before, /device:TPU:8 now
where the time goes in v1:
time: 113 us
  starting transfers between devices  36.6 us (32%)
  waiting for transfers between devices  32.3 us (29%)
  blocking collectives  23.1 us (20%)
  Pallas kernels  13.5 us (12%)
  other arithmetic  3.37 us (3%)
  local copies, waits for them, and re-layouts  3.25 us (3%)
    ppermute x7, starting transfers between devices, shifted(): return lax.ppermute(x, axis, [(i, (i + step) % size) for i in range(size)])  32.3 us
    ppermute x7, waiting for transfers between devices, shifted(): return lax.ppermute(x, axis, [(i, (i + step) % size) for i in range(size)])  27.2 us
    all_to_all x1, blocking collectives, copy_for_each(): lax.all_to_all(jnp.broadcast_to(x[None], (size, *x.shape)), axis, 0, 0, t...  14 us
    pallas_call x1, Pallas kernels, head(): pl.pallas_call(kernel, out_shape=(jax.ShapeDtypeStruct((length, D_VAL), b...  13.5 us
    all_to_all x1, blocking collectives, local(): parts = lax.all_to_all(grad, 'x', 0, 0, tiled=True)  9.07 us
    all_to_all x1, waiting for transfers between devices, copy_for_each(): lax.all_to_all(jnp.broadcast_to(x[None], (size, *x.shape)), axis, 0, 0, t...  5.13 us
    all_to_all x1, starting transfers between devices, copy_for_each(): lax.all_to_all(jnp.broadcast_to(x[None], (size, *x.shape)), axis, 0, 0, t...  4.29 us
  transfers between devices with their start and end apart: 8, of which 6 were waited for; matrix products, arithmetic and copies ran while one was open for 2% of the time, Pallas kernels for 0%

profile of v1, /device:TPU:8, one launch (start us, length us, event | category | flops | bytes accessed | tf_op | source)
XLA Modules:
  0.0 112.9 jit_solution(617727685488598575)
XLA Ops:
  0.6 0.9 fusion.1
  1.5 0.7 slice.21
  2.2 0.7 convert_bitcast_fusion
  2.9 0.8 fusion.3
  3.9 14.0 %all_to_all.15 = bf16[4,32,640]{2,1,0:T(8,128)(2,1)S(1)} all-to-all(bf16[4,32,640]{2,1,0:T(8,128)(2,1)S(1)} %broadcast_in_dim.9), channel_id=1, replica_groups=mesh['zh'=2,'x'=4,'zl'=4,'y'=8,'c'=2] {'zl'}, dimensions={0} | all-to-all | bytes 327680 | tf_op jit(solution)/shard_map/all_to_all | solution.py:37
  17.9 6.7 %collective-permute-start = (bf16[128,640]{1,0:T(8,128)(2,1)S(1)}, bf16[128,640]{1,0:T(8,128)(2,1)S(1)}, u32[]{:S(2)}, u32[]{:S(2)}) collective-permute-start(bf16[128,640]{1,0:T(8,128)(2,1)S(1)} %bitcast.28), channel_id=1, source_target_pairs={{0,6},{2,8},{4,10},{6,12},{8,14},{10,0},{12,2},{14,4},{1,7},{3,9},... | collective-permute-start | bytes 491528 | tf_op jit(solution)/shard_map/ppermute | solution.py:32
  24.6 2.1 %collective-permute-start.1 = (bf16[128,640]{1,0:T(8,128)(2,1)S(1)}, bf16[128,640]{1,0:T(8,128)(2,1)S(1)}, u32[]{:S(2)}, u32[]{:S(2)}) collective-permute-start(bf16[128,640]{1,0:T(8,128)(2,1)S(1)} %bitcast.29), channel_id=1, source_target_pairs={{0,10},{2,12},{4,14},{6,0},{8,2},{10,4},{12,6},{14,8},{1,11},{3,13... | collective-permute-start | bytes 491528 | tf_op jit(solution)/shard_map/ppermute | solution.py:32
  26.8 7.5 %collective-permute-done = bf16[128,640]{1,0:T(8,128)(2,1)S(1)} collective-permute-done((bf16[128,640]{1,0:T(8,128)(2,1)S(1)}, bf16[128,640]{1,0:T(8,128)(2,1)S(1)}, u32[]{:S(2)}, u32[]{:S(2)}) %collective-permute-start) | collective-permute-done | bytes 163872 | tf_op jit(solution)/shard_map/ppermute | solution.py:32
  34.2 6.4 %collective-permute-done.1 = bf16[128,640]{1,0:T(8,128)(2,1)S(1)} collective-permute-done((bf16[128,640]{1,0:T(8,128)(2,1)S(1)}, bf16[128,640]{1,0:T(8,128)(2,1)S(1)}, u32[]{:S(2)}, u32[]{:S(2)}) %collective-permute-start.1) | collective-permute-done | bytes 163872 | tf_op jit(solution)/shard_map/ppermute | solution.py:32
  40.7 1.9 %collective-permute-start.2 = (bf16[384,640]{1,0:T(8,128)(2,1)S(1)}, bf16[384,640]{1,0:T(8,128)(2,1)S(1)}, u32[]{:S(2)}, u32[]{:S(2)}) collective-permute-start(bf16[384,640]{1,0:T(8,128)(2,1)S(1)} %pad_maximum_fusion), channel_id=1, source_target_pairs={{0,2},{2,4},{4,6},{6,8},{8,10},{10,12},{12,14},{14,0},{1,3},{3,5},... | collective-permute-start | bytes 1474568 | tf_op jit(solution)/shard_map/ppermute | solution.py:32
  42.7 3.9 %collective-permute-start.3 = (bf16[256,640]{1,0:T(8,128)(2,1)S(1)}, bf16[256,640]{1,0:T(8,128)(2,1)S(1)}, u32[]{:S(2)}, u32[]{:S(2)}) collective-permute-start(bf16[256,640]{1,0:T(8,128)(2,1)S(1)} %pad_maximum_fusion.1), channel_id=1, source_target_pairs={{0,14},{2,0},{4,2},{6,4},{8,6},{10,8},{12,10},{14,12},{1,15},{3,1}... | collective-permute-start | bytes 983048 | tf_op jit(solution)/shard_map/ppermute | solution.py:32
  46.7 8.8 %collective-permute-done.2 = bf16[384,640]{1,0:T(8,128)(2,1)S(1)} collective-permute-done((bf16[384,640]{1,0:T(8,128)(2,1)S(1)}, bf16[384,640]{1,0:T(8,128)(2,1)S(1)}, u32[]{:S(2)}, u32[]{:S(2)}) %collective-permute-start.2) | collective-permute-done | bytes 491552 | tf_op jit(solution)/shard_map/ppermute | solution.py:32
  55.6 1.9 %collective-permute-start.4 = (bf16[1024,640]{1,0:T(8,128)(2,1)S(1)}, bf16[1024,640]{1,0:T(8,128)(2,1)}, u32[]{:S(2)}, u32[]{:S(2)}) collective-permute-start(bf16[1024,640]{1,0:T(8,128)(2,1)S(1)} %constant_dynamic-update-slice_fusion.mine), channel_id=1, source_target_pairs={{0,1},{1,0},{2,3},{3,2},{4,5},{5,4},{6,7},{7,6},{8,9},{9,8},{10,11... | collective-permute-start | bytes 3932168 | tf_op jit(solution)/shard_map/ppermute | solution.py:32
  57.5 8.3 %collective-permute-start.5 = (bf16[64,256]{1,0:T(8,128)(2,1)S(1)}, bf16[64,256]{1,0:T(8,128)(2,1)S(1)}, u32[]{:S(2)}, u32[]{:S(2)}) collective-permute-start(bf16[64,256]{1,0:T(8,128)(2,1)S(1)} %copy-done.5), channel_id=1, source_target_pairs={{0,256},{256,0},{1,257},{257,1},{2,258},{258,2},{3,259},{259,3},{4... | collective-permute-start | bytes 98312 | tf_op jit(solution)/shard_map/ppermute | solution.py:32
  65.8 2.0 %collective-permute-done.5 = bf16[64,256]{1,0:T(8,128)(2,1)S(1)} collective-permute-done((bf16[64,256]{1,0:T(8,128)(2,1)S(1)}, bf16[64,256]{1,0:T(8,128)(2,1)S(1)}, u32[]{:S(2)}, u32[]{:S(2)}) %collective-permute-start.5) | collective-permute-done | bytes 32800 | tf_op jit(solution)/shard_map/ppermute | solution.py:32
  67.9 0.7 broadcast_in_dim.10
  68.6 4.3 %all-to-all-start.1 = ((bf16[4,2,64,256]{3,2,1,0:T(8,128)(2,1)}), bf16[4,2,64,256]{3,2,1,0:T(8,128)(2,1)S(1)}, u32[]{:S(2)}, u32[]{:S(2)}) async-start(bf16[4,2,64,256]{3,2,1,0:T(8,128)(2,1)} %broadcast_in_dim.10), calls=%async_computation.1 | async-start | bytes 524288 | tf_op jit(solution)/shard_map/all_to_all | solution.py:37
  72.9 1.5 %copy.13 = bf16[1,2048,192]{2,1,0:T(8,128)(2,1)S(1)} copy(bf16[1,2048,192]{1,2,0:T(8,128)(2,1)} %param.10) | data formatting | bytes 1572864 | tf_op args[0]
  74.5 5.1 %all-to-all-done.1 = bf16[4,2,64,256]{3,2,1,0:T(8,128)(2,1)S(1)} async-done(((bf16[4,2,64,256]{3,2,1,0:T(8,128)(2,1)}), bf16[4,2,64,256]{3,2,1,0:T(8,128)(2,1)S(1)}, u32[]{:S(2)}, u32[]{:S(2)}) %all-to-all-start.1) | async-done | bytes 262176 | tf_op jit(solution)/shard_map/all_to_all | solution.py:37
  79.8 13.5 %head.1 = (bf16[2048,128]{1,0:T(8,128)(2,1)}, bf16[512,256]{1,0:T(8,128)(2,1)S(1)}) custom-call(s32[2]{0:T(128)S(1)} %pad_add_fusion.place, bf16[1024,640]{1,0:T(8,128)(2,1)S(1)} %constant_dynamic-update-slice_fusion.mine, bf16[1024,640]{1,0:T(8,128)(2,1)} %collective-permute-done.4.other, bf16[2048,192]{1,0:T(8,128)(2,1)S(1)} %bitcast.24, ...), custom_call_target="tpu_custom_call" | custom-call | tf_op jit(solution)/shard_map/head/pallas_call | solution.py:210
  93.3 9.1 %all_to_all.16 = bf16[4,2,64,256]{3,2,1,0:T(8,128)(2,1)S(1)} all-to-all(bf16[4,2,64,256]{3,2,1,0:T(8,128)(2,1)S(1)} %bitcast.33), channel_id=1, replica_groups=mesh['zh'=2,'x'=4,'zl'=4,'y'=8,'c'=2] {'x'}, dimensions={0} | all-to-all | bytes 524288 | tf_op jit(solution)/shard_map/all_to_all | solution.py:260
  102.4 7.4 %collective-permute-start.6 = (bf16[64,256]{1,0:T(8,128)(2,1)S(1)}, bf16[64,256]{1,0:T(8,128)(2,1)S(1)}, u32[]{:S(2)}, u32[]{:S(2)}) collective-permute-start(bf16[64,256]{1,0:T(8,128)(2,1)S(1)} %fusion.5), channel_id=1, source_target_pairs={{0,256},{256,0},{1,257},{257,1},{2,258},{258,2},{3,259},{259,3},{4... | collective-permute-start | bytes 98312 | tf_op jit(solution)/shard_map/ppermute | solution.py:32
  109.8 2.5 %collective-permute-done.6 = bf16[64,256]{1,0:T(8,128)(2,1)S(1)} collective-permute-done((bf16[64,256]{1,0:T(8,128)(2,1)S(1)}, bf16[64,256]{1,0:T(8,128)(2,1)S(1)}, u32[]{:S(2)}, u32[]{:S(2)}) %collective-permute-start.6) | collective-permute-done | bytes 32800 | tf_op jit(solution)/shard_map/ppermute | solution.py:32
  112.3 0.7 fusion.4
  (32 shorter events, 0.7 us)
Async XLA Ops:
  17.9 16.3 %collective-permute-start = (bf16[128,640]{1,0:T(8,128)(2,1)S(1)}, bf16[128,640]{1,0:T(8,128)(2,1)S(1)}, u32[]{:S(2)}, u32[]{:S(2)}) collective-permute-start(bf16[128,640]{1,0:T(8,128)(2,1)S(1)} %bitcast.28), channel_id=1, source_target_pairs={{0,6},{2,8},{4,10},{6,12},{8,14},{10,0},{12,2},{14,4},{1,7},{3,9},... | collective-permute-start | bytes 491528 | tf_op jit(solution)/shard_map/ppermute | solution.py:32
  24.6 16.0 %collective-permute-start.1 = (bf16[128,640]{1,0:T(8,128)(2,1)S(1)}, bf16[128,640]{1,0:T(8,128)(2,1)S(1)}, u32[]{:S(2)}, u32[]{:S(2)}) collective-permute-start(bf16[128,640]{1,0:T(8,128)(2,1)S(1)} %bitcast.29), channel_id=1, source_target_pairs={{0,10},{2,12},{4,14},{6,0},{8,2},{10,4},{12,6},{14,8},{1,11},{3,13... | collective-permute-start | bytes 491528 | tf_op jit(solution)/shard_map/ppermute | solution.py:32
  40.7 14.8 %collective-permute-start.2 = (bf16[384,640]{1,0:T(8,128)(2,1)S(1)}, bf16[384,640]{1,0:T(8,128)(2,1)S(1)}, u32[]{:S(2)}, u32[]{:S(2)}) collective-permute-start(bf16[384,640]{1,0:T(8,128)(2,1)S(1)} %pad_maximum_fusion), channel_id=1, source_target_pairs={{0,2},{2,4},{4,6},{6,8},{8,10},{10,12},{12,14},{14,0},{1,3},{3,5},... | collective-permute-start | bytes 1474568 | tf_op jit(solution)/shard_map/ppermute | solution.py:32
  42.7 14.9 %copy-start.5 = (bf16[64,256]{1,0:T(8,128)(2,1)S(1)}, bf16[64,256]{1,0:T(8,128)(2,1)}, u32[]{:S(2)}) copy-start(bf16[64,256]{1,0:T(8,128)(2,1)} %param.14) | copy-start | bytes 98308
  42.7 12.9 %collective-permute-start.3 = (bf16[256,640]{1,0:T(8,128)(2,1)S(1)}, bf16[256,640]{1,0:T(8,128)(2,1)S(1)}, u32[]{:S(2)}, u32[]{:S(2)}) collective-permute-start(bf16[256,640]{1,0:T(8,128)(2,1)S(1)} %pad_maximum_fusion.1), channel_id=1, source_target_pairs={{0,14},{2,0},{4,2},{6,4},{8,6},{10,8},{12,10},{14,12},{1,15},{3,1}... | collective-permute-start | bytes 983048 | tf_op jit(solution)/shard_map/ppermute | solution.py:32
  55.6 24.1 %collective-permute-start.4 = (bf16[1024,640]{1,0:T(8,128)(2,1)S(1)}, bf16[1024,640]{1,0:T(8,128)(2,1)}, u32[]{:S(2)}, u32[]{:S(2)}) collective-permute-start(bf16[1024,640]{1,0:T(8,128)(2,1)S(1)} %constant_dynamic-update-slice_fusion.mine), channel_id=1, source_target_pairs={{0,1},{1,0},{2,3},{3,2},{4,5},{5,4},{6,7},{7,6},{8,9},{9,8},{10,11... | collective-permute-start | bytes 3932168 | tf_op jit(solution)/shard_map/ppermute | solution.py:32
  57.5 10.3 %collective-permute-start.5 = (bf16[64,256]{1,0:T(8,128)(2,1)S(1)}, bf16[64,256]{1,0:T(8,128)(2,1)S(1)}, u32[]{:S(2)}, u32[]{:S(2)}) collective-permute-start(bf16[64,256]{1,0:T(8,128)(2,1)S(1)} %copy-done.5), channel_id=1, source_target_pairs={{0,256},{256,0},{1,257},{257,1},{2,258},{258,2},{3,259},{259,3},{4... | collective-permute-start | bytes 98312 | tf_op jit(solution)/shard_map/ppermute | solution.py:32
  68.6 11.0 %all-to-all-start.1 = ((bf16[4,2,64,256]{3,2,1,0:T(8,128)(2,1)}), bf16[4,2,64,256]{3,2,1,0:T(8,128)(2,1)S(1)}, u32[]{:S(2)}, u32[]{:S(2)}) async-start(bf16[4,2,64,256]{3,2,1,0:T(8,128)(2,1)} %broadcast_in_dim.10), calls=%async_computation.1 | async-start | bytes 524288 | tf_op jit(solution)/shard_map/all_to_all | solution.py:37
  72.9 6.8 %copy-start = (bf16[1,2048,128]{2,1,0:T(8,128)(2,1)S(1)}, bf16[1,2048,128]{2,1,0:T(8,128)(2,1)}, u32[]{:S(2)}) copy-start(bf16[1,2048,128]{2,1,0:T(8,128)(2,1)} %param.15) | copy-start | bytes 1572868
  72.9 6.8 %copy-start.1 = (f32[256,256]{1,0:T(8,128)S(1)}, f32[256,256]{1,0:T(8,128)}, u32[]{:S(2)}) copy-start(f32[256,256]{1,0:T(8,128)} %constant.32.clone.table) | copy-start | bytes 786436
  72.9 6.9 %copy-start.2 = (bf16[128,384]{1,0:T(8,128)(2,1)S(1)}, bf16[128,384]{1,0:T(8,128)(2,1)}, u32[]{:S(2)}) copy-start(bf16[128,384]{1,0:T(8,128)(2,1)} %constant.33.clone.pick) | copy-start | bytes 294916
  72.9 6.9 %copy-start.3 = (f32[1,128]{1,0:T(1,128)S(1)}, f32[1,128]{1,0:T(1,128)}, u32[]{:S(2)}) copy-start(f32[1,128]{1,0:T(1,128)} %constant.31.clone.freq) | copy-start | bytes 1540
  93.2 19.1 %copy-start.4 = (f32[64,256]{1,0:T(8,128)S(1)}, f32[64,256]{1,0:T(8,128)}, u32[]{:S(2)}) copy-start(f32[64,256]{1,0:T(8,128)} %param.16) | copy-start | bytes 196612
  102.4 9.9 %collective-permute-start.6 = (bf16[64,256]{1,0:T(8,128)(2,1)S(1)}, bf16[64,256]{1,0:T(8,128)(2,1)S(1)}, u32[]{:S(2)}, u32[]{:S(2)}) collective-permute-start(bf16[64,256]{1,0:T(8,128)(2,1)S(1)} %fusion.5), channel_id=1, source_target_pairs={{0,256},{256,0},{1,257},{257,1},{2,258},{258,2},{3,259},{259,3},{4... | collective-permute-start | bytes 98312 | tf_op jit(solution)/shard_map/ppermute | solution.py:32

commit v2 on v1

--- a/solution.py
+++ b/solution.py
@@ -37,10 +37,47 @@
     return lax.all_to_all(jnp.broadcast_to(x[None], (size, *x.shape)), axis, 0, 0, tiled=True)
 
 
-def normalize(latent_rows, latent_gain):
-    compressed = latent_rows[:, :D_LAT].astype(f32)
+def row_kernel(latent_in, gain_in, numbers_in, out, latent, gain, numbers, arrived):
+    rows = latent.shape[0]
+    copies = [
+        pltpu.make_async_copy(source, target, arrived.at[i])
+        for i, (source, target) in enumerate(
+            ((latent_in, latent), (gain_in, gain), (numbers_in, numbers))
+        )
+    ]
+    for copy in copies:
+        copy.start()
+    for copy in copies:
+        copy.wait()
+    compressed = latent[:, :D_LAT].astype(f32)
     spread = jnp.mean(compressed * compressed, axis=-1, keepdims=True)
-    return (compressed * lax.rsqrt(spread + epsilon) * latent_gain).astype(bf16)
+    normed = (compressed * lax.rsqrt(spread + epsilon) * gain[...]).astype(bf16)
+    at = lax.broadcasted_iota(jnp.int32, (rows, rows), 0)
+    across = lax.broadcasted_iota(jnp.int32, (rows, rows), 1)
+    spread_out = jnp.broadcast_to(numbers[...], (rows, rows))
+    number = jnp.sum(jnp.where(at == across, spread_out, 0).astype(f32), axis=1, keepdims=True)
+    tail = jnp.broadcast_to(number, (rows, D_ROW - D_LAT - D_ROPE)).astype(bf16)
+    rope = jnp.concatenate([latent[:, D_LAT:], tail], axis=1)
+    for i in range(out.shape[0]):
+        out[i, :, :D_LAT] = normed
+        out[i, :, D_LAT:] = rope
+
+
+def rows_to_send(latent, latent_gain, segments, copies):
+    return pl.pallas_call(
+        row_kernel,
+        out_shape=jax.ShapeDtypeStruct((copies, latent.shape[0], D_ROW), bf16),
+        in_specs=[pl.BlockSpec(memory_space=pltpu.HBM)] * 3,
+        out_specs=pl.BlockSpec(memory_space=pltpu.VMEM),
+        scratch_shapes=[
+            pltpu.VMEM(latent.shape, bf16),
+            pltpu.VMEM((1, D_LAT), f32),
+            pltpu.VMEM(segments.shape, jnp.int32),
+            pltpu.SemaphoreType.DMA((3,)),
+        ],
+        compiler_params=pltpu.CompilerParams(vmem_limit_bytes=4 * 1024 * 1024),
+        name="rows",
+    )(latent, latent_gain[None], segments)
 
 
 def nt(a, b):
@@ -55,52 +92,109 @@
     return lax.dot_general(a, b, (((0,), (0,)), ((), ())), preferred_element_type=f32)
 
 
-Y_OFFSETS = (-3, 0, 3, -4, -1, 2, -2, 1)
+NEAR = tuple((away, z) for away in (-3, 0, 3) for z in range(4))
+FAR = (
+    (-4, 2), (-4, 3),
+    *((away, z) for away in (-1, 2, -2, 1) for z in range(4)),
+    (-4, 0), (-4, 1),
+)
 
 
 def constants():
     half = D_ROPE // 2
     freq = rope_base ** (-(2.0 * np.arange(half)) / D_ROPE)
-    freq_row = np.zeros((1, 128), np.float32)
-    freq_row[0, :half] = freq
-    freq_row[0, half:D_ROPE] = freq
-    angles = np.arange(BLOCK)[:, None] * np.concatenate([freq, freq])[None, :]
-    table = np.zeros((BLOCK, 256), np.float32)
-    table[:, :D_ROPE] = np.cos(angles)
-    table[:, 128 : 128 + D_ROPE] = np.sin(angles)
-    pick = np.zeros((128, 384), np.float32)
-    for i in range(half):
-        pick[i, i] = 1.0
-        pick[half + i, half + i] = 1.0
-        pick[half + i, 128 + i] = -1.0
-        pick[i, 128 + half + i] = 1.0
-    pick[D_ROPE, 256:] = 1.0
-    return freq_row, table, pick
+    twice = np.concatenate([freq, freq])
+    angles = np.arange(BLOCK)[:, None] * twice[None, :]
+    table = np.zeros((BLOCK + 8, 256), np.float32)
+    table[:BLOCK, :D_ROPE] = np.cos(angles)
+    table[:BLOCK, 128 : 128 + D_ROPE] = np.sin(angles)
+    table[BLOCK:, :D_ROPE] = twice
+    return table
+
+
+def picker(size):
+    row = lax.broadcasted_iota(jnp.int32, (size, 256), 0)
+    lane = lax.broadcasted_iota(jnp.int32, (size, 256), 1)
+    half = D_ROPE // 2
+    same = (lane == row) & (row < D_ROPE)
+    plus = (lane == row + 128 + half) & (row < half)
+    minus = (lane == row + 128 - half) & (row >= half) & (row < D_ROPE)
+    return jnp.where(same | plus, 1.0, jnp.where(minus, -1.0, 0.0)).astype(bf16)
+
+
+def stage_kernel(queries_in, grads_in, table_in, parts, grads, table, queries, arrived):
+    copies = [
+        pltpu.make_async_copy(source, target, arrived.at[i])
+        for i, (source, target) in enumerate(
+            ((queries_in, queries), (grads_in, grads), (table_in, table))
+        )
+    ]
+    for copy in copies:
+        copy.start()
+    pick = picker(D_ROPE)
+    copies[0].wait()
+    for i in range(parts.shape[0] // BLOCK):
+        rows = slice(i * BLOCK, (i + 1) * BLOCK)
+        parts[rows, :D_NOPE] = queries[:D_NOPE, rows].T
+        parts[rows, D_NOPE:] = tn(queries[D_NOPE:, rows], pick).astype(bf16)
+    copies[1].wait()
+    copies[2].wait()
+
+
+def staged(queries, grads):
+    table = jnp.asarray(constants())
+    length = grads.shape[0]
+    return pl.pallas_call(
+        stage_kernel,
+        out_shape=(
+            jax.ShapeDtypeStruct((length, D_NOPE + 256), bf16),
+            jax.ShapeDtypeStruct(grads.shape, bf16),
+            jax.ShapeDtypeStruct(table.shape, f32),
+        ),
+        in_specs=[pl.BlockSpec(memory_space=pltpu.HBM)] * 3,
+        out_specs=(pl.BlockSpec(memory_space=pltpu.VMEM),) * 3,
+        scratch_shapes=[pltpu.VMEM(queries.shape, bf16), pltpu.SemaphoreType.DMA((3,))],
+        compiler_params=pltpu.CompilerParams(vmem_limit_bytes=8 * 1024 * 1024),
+        cost_estimate=pl.CostEstimate(flops=400_000_000, bytes_accessed=4_000_000, transcendentals=0),
+        name="stage",
+    )(queries, grads, table)
 
 
 def kernel(
-    place, mine, other, queries, grads, weight, freq, table, pick,
+    place, near, far, near_other, far_other, query_parts, grads, table, pieces,
     out, gradient,
-    lat, hot, key, query, val, val_t, starts, key_grad, val_grad, firsts,
+    result_rows,
+    weight, lat, hot, key, query, val, val_t, starts, key_grad, val_grad, firsts, left,
 ):
     length = lat.shape[0]
     blocks = length // BLOCK
     y, c = place[0], place[1]
-    own = mine.shape[0] // (4 * 8)
-    for z in range(4):
-        for j, away in enumerate(Y_OFFSETS):
-            at = (z * 8 + lax.rem(y + (away + 8), 8)) * (2 * own)
-            rows = slice((j * 4 + z) * own, (j * 4 + z + 1) * own)
-            lat[pl.ds(pl.multiple_of(at + c * own, own), own), :] = mine[rows, :]
-            lat[pl.ds(pl.multiple_of(at + (1 - c) * own, own), own), :] = other[rows, :]
+    own = near.shape[0] // len(NEAR)
+
+    def put(source, held, core):
+        for k, (away, z) in enumerate(held):
+            at = ((z * 8 + lax.rem(y + (away + 8), 8)) * 2 + core) * own
+            lat[pl.ds(pl.multiple_of(at, own), own), :] = source[k * own : (k + 1) * own, :]
+
+    put(near, NEAR, c)
+    put(far, FAR, c)
+    put(far_other, FAR, 1 - c)
+    put(near_other, NEAR, 1 - c)
+    share = pieces.shape[2]
+    for x in range(4):
+        for k in range(2):
+            at = ((place[2] ^ k) * 4 + x) * share
+            weight[pl.ds(pl.multiple_of(at, share), share), :] = pieces[x, k]
 
     lane = lax.broadcasted_iota(jnp.int32, (BLOCK, 128), 1)
     row = lax.broadcasted_iota(jnp.int32, (BLOCK, 128), 0)
     doc = (lane & 7).astype(f32)
+    pick = picker(128)
+    spread = jnp.where(row[:128] == D_ROPE, 1.0, 0.0).astype(bf16)
     first = jnp.full((1, 128), 8192, jnp.int32)
     for i in range(blocks):
         at = i * BLOCK
-        number = nn(lat[at : at + BLOCK, D_LAT:], pick[:, 256:])
+        number = nn(lat[at : at + BLOCK, D_LAT:], spread)
         here = number == doc
         hot[at : at + BLOCK, :] = jnp.where(here, 1.0, 0.0).astype(bf16)
         first = jnp.minimum(
@@ -114,7 +208,8 @@
     split = jnp.where(lane8 < 8, first8 - low, jnp.where(lane8 < 16, low, 0))
     split = split.astype(f32).astype(bf16)
 
-    @pl.loop(0, blocks)
+
+    @pl.loop(0, blocks, unroll=2)
     def prepare(i):
         at = pl.multiple_of(i * BLOCK, BLOCK)
         rows = pl.ds(at, BLOCK)
@@ -122,7 +217,7 @@
         begun = nt(split, marks)
         starts[:, rows] = begun
         firsts[i] = begun[0, 0].astype(jnp.int32)
-        theta = (column - lax.convert_element_type(at, f32)) * freq[...]
+        theta = (column - lax.convert_element_type(at, f32)) * table[BLOCK:, :128]
         both = jnp.concatenate([jnp.cos(theta), jnp.sin(theta)], axis=1)
         high = both.astype(bf16).astype(f32)
         middle = (both - high).astype(bf16).astype(f32)
@@ -130,13 +225,13 @@
         parts = jnp.concatenate([high, middle, last, jnp.zeros_like(both)], axis=0).astype(bf16)
         turn = nn(marks[:, :32], parts)
         cos_s, sin_s = turn[:, :128], turn[:, 128:]
-        cos_b, sin_b = table[:, :128], table[:, 128:]
+        cos_b, sin_b = table[:BLOCK, :128], table[:BLOCK, 128:]
         cosine = cos_b * cos_s + sin_b * sin_s
         sine = sin_b * cos_s - cos_b * sin_s
-        raw = nn(lat[rows, D_LAT:], pick[:, :256])
+        raw = nn(lat[rows, D_LAT:], pick)
         key[rows, D_NOPE:] = (raw[:, :128] * cosine + raw[:, 128:] * sine).astype(bf16)
-        raw = nn(queries[rows, D_NOPE:], pick[:D_ROPE, :256])
-        query[rows, :D_NOPE] = queries[rows, :D_NOPE]
+        raw = query_parts[rows, D_NOPE:].astype(f32)
+        query[rows, :D_NOPE] = query_parts[rows, :D_NOPE]
         query[rows, D_NOPE:] = (raw[:, :128] * cosine + raw[:, 128:] * sine).astype(bf16)
         pair = nn(lat[rows, :D_LAT], weight[...])
         key[rows, :D_NOPE] = pair[:, :D_NOPE].astype(bf16)
@@ -182,7 +277,8 @@
             val_grad[span, :] += nn(lows[j], grad)
             score_grad = (probs[j] * (prob_grads[j] - delta)).astype(bf16)
             key_grad[span, :] += nn(score_grad, q_full[:, :D_NOPE])
-        out[rows, :] = result.T.astype(bf16)
+        result_rows[rows, :] = result.T.astype(bf16)
+        pltpu.make_async_copy(result_rows.at[rows, :], out.at[rows, :], left.at[i]).start()
 
     @pl.loop(0, blocks)
     def attention(i):
@@ -200,22 +296,26 @@
         rows = slice(i * BLOCK, (i + 1) * BLOCK)
         columns = jnp.concatenate([key_grad[rows, :] * score_scale, val_grad[rows, :]], axis=1)
         total = total + tn(lat[rows, :D_LAT], columns.astype(bf16))
-    gradient[...] = total.astype(bf16)
-
-
-def head(place, mine, other, queries, grads, weight):
-    length = queries.shape[0]
-    freq, table, pick = constants()
+    gradient[...] = total.astype(bf16).reshape(gradient.shape)
+    for i in range(blocks):
+        rows = pl.ds(i * BLOCK, BLOCK)
+        pltpu.make_async_copy(result_rows.at[rows, :], out.at[rows, :], left.at[i]).wait()
+
+
+def head(place, near, far, near_other, far_other, query_parts, grads, table, pieces):
+    length = grads.shape[0]
     vmem = pl.BlockSpec(memory_space=pltpu.VMEM)
     return pl.pallas_call(
         kernel,
         out_shape=(
             jax.ShapeDtypeStruct((length, D_VAL), bf16),
-            jax.ShapeDtypeStruct((D_LAT, D_NOPE + D_VAL), bf16),
+            jax.ShapeDtypeStruct((8, D_LAT // 8, D_NOPE + D_VAL), bf16),
         ),
         in_specs=[pl.BlockSpec(memory_space=pltpu.SMEM)] + [vmem] * 8,
-        out_specs=(vmem, vmem),
+        out_specs=(pl.BlockSpec(memory_space=pltpu.HBM), vmem),
         scratch_shapes=[
+            pltpu.VMEM((length, D_VAL), bf16),
+            pltpu.VMEM((D_LAT, D_NOPE + D_VAL), bf16),
             pltpu.VMEM((length, D_ROW), bf16),
             pltpu.VMEM((length, 128), bf16),
             pltpu.VMEM((length, 256), bf16),
@@ -226,41 +326,35 @@
             pltpu.VMEM((length, D_NOPE), f32),
             pltpu.VMEM((length, D_VAL), f32),
             pltpu.SMEM((length // BLOCK,), jnp.int32),
+            pltpu.SemaphoreType.DMA((length // BLOCK,)),
         ],
-        compiler_params=pltpu.CompilerParams(vmem_limit_bytes=48 * 1024 * 1024),
+        compiler_params=pltpu.CompilerParams(vmem_limit_bytes=18 * 1024 * 1024),
+        cost_estimate=pl.CostEstimate(flops=3_000_000_000, bytes_accessed=8_000_000, transcendentals=2_000_000),
         name="head",
-    )(place, mine, other, queries, grads, weight, jnp.asarray(freq), jnp.asarray(table), jnp.asarray(pick, bf16))
+    )(place, near, far, near_other, far_other, query_parts, grads, table, pieces)
 
 
 def local(queries, latent, latent_gain, segments, up_weight, out_grad, hess_old):
-    rows = latent.shape[1]
-    normed = normalize(latent[0], latent_gain)
-    number = jnp.broadcast_to(segments[0][:, None], (rows, D_ROW - D_LAT - D_ROPE)).astype(bf16)
-    mine = jnp.concatenate([normed, latent[0][:, D_LAT:], number], axis=1)
-
-    weight = jnp.stack([up_weight, shifted(up_weight, "zh", 1)])
-    line = copy_for_each(mine, "zl").reshape(-1, D_ROW)
+    up = lax.axis_index("zh")
+    place = jnp.stack([lax.axis_index("y"), lax.axis_index("c"), up]).astype(jnp.int32)
+    weight = shifted(up_weight, "zh", 1)
+    sent = rows_to_send(latent[0], latent_gain, segments, 4)
+    line = lax.all_to_all(sent, "zl", 0, 0, tiled=True).reshape(-1, D_ROW)
     upper = shifted(line, "y", 3)
     lower = shifted(line, "y", -3)
-    three = jnp.concatenate([upper, line, lower], axis=0)
-    left = shifted(three, "y", 1)
-    right = shifted(three[: 2 * line.shape[0]], "y", -1)
-    half = jnp.concatenate([three, left, right], axis=0)
-    other = shifted(half, "c", 1)
+    weight = jnp.stack([up_weight, weight])
     weight = copy_for_each(weight, "x")
-    up = lax.axis_index("zh")
-    weight = jnp.where(up == 0, weight, weight[:, ::-1])
-    weight = jnp.swapaxes(weight, 0, 1).reshape(D_LAT, D_NOPE + D_VAL)
-
-    place = jnp.stack([lax.axis_index("y"), lax.axis_index("c")]).astype(jnp.int32)
-    attn_out, grad = head(place, half, other, queries[0], out_grad[0], weight)
-
-    share = hess_old.shape[0]
-    grad = jnp.swapaxes(grad.reshape(2, 4, share, -1), 0, 1)
-    parts = lax.all_to_all(grad, "x", 0, 0, tiled=True)
-    summed = jnp.sum(parts.astype(f32), axis=0)
-    sent = shifted(jnp.where(up == 0, summed[1], summed[0]).astype(bf16), "zh", 1)
-    total = jnp.where(up == 0, summed[0], summed[1]) + sent.astype(f32)
+    near = jnp.concatenate([upper, line, lower], axis=0)
+    near, weight = lax.optimization_barrier((near, weight))
+    left = shifted(near[line.shape[0] // 2 :], "y", 1)
+    right = shifted(near[: 5 * line.shape[0] // 2], "y", -1)
+    near_other = shifted(near, "c", 1)
+    far = jnp.concatenate([left, right], axis=0)
+    far_other = shifted(far, "c", 1)
+    ready = staged(queries[0].T, out_grad[0])
+    attn_out, grad = head(place, near, far, near_other, far_other, *ready, weight)
+    parts = lax.all_to_all(grad, DP, 0, 0, tiled=True)
+    total = sum(parts[i].astype(f32) for i in range(parts.shape[0]))
     hess_new = ema_decay * hess_old + (1.0 - ema_decay) * total * total
     return (attn_out[None], hess_new)
 

time: 113 us -> 95.9 us (0.85)
  the two profiles are of different devices: /device:TPU:8 before, /device:TPU:56 now
where the time goes in v2:
time: 95.9 us; the launch traced here: 95.2 us
  starting transfers between devices  39.1 us (41%)
  waiting for transfers between devices  19.7 us (21%)
  blocking collectives  17.8 us (19%)
  Pallas kernels  13.3 us (14%)
  local copies, waits for them, and re-layouts  3 us (3%)
  other arithmetic  1.57 us (2%)
    ppermute x7, starting transfers between devices, shifted(): return lax.ppermute(x, axis, [(i, (i + step) % size) for i in range(size)])  27.5 us
    all_to_all x1, blocking collectives, local(): parts = lax.all_to_all(grad, DP, 0, 0, tiled=True)  17.8 us
    ppermute x7, waiting for transfers between devices, shifted(): return lax.ppermute(x, axis, [(i, (i + step) % size) for i in range(size)])  16.9 us
    pallas_call x1, Pallas kernels, head(): pl.pallas_call(kernel, out_shape=(jax.ShapeDtypeStruct((length, D_VAL), b...  11.9 us
    all_to_all x1, starting transfers between devices, local(): line = lax.all_to_all(sent, 'zl', 0, 0, tiled=True).reshape(-1, D_ROW)  7.27 us
    all_to_all x1, starting transfers between devices, copy_for_each(): lax.all_to_all(jnp.broadcast_to(x[None], (size, *x.shape)), axis, 0, 0, t...  4.29 us
    all_to_all x1, waiting for transfers between devices, copy_for_each(): lax.all_to_all(jnp.broadcast_to(x[None], (size, *x.shape)), axis, 0, 0, t...  2.78 us
    unnamed x15, local copies, waits for them, and re-layouts  2.17 us
  transfers between devices with their start and end apart: 9, of which 6 were waited for; matrix products, arithmetic and copies ran while one was open for 2% of the time, Pallas kernels for 1%

profile of v2, /device:TPU:56, one launch (start us, length us, event | category | flops | bytes accessed | tf_op | source)
XLA Modules:
  0.0 95.2 jit_solution(17302902509014449277)
XLA Ops:
  0.6 0.8 copy-done.3
  1.4 0.7 copy-done.4
  2.1 0.7 copy-done.5
  2.7 0.8 rows.1
  3.6 7.3 %all-to-all-start = ((bf16[4,32,640]{2,1,0:T(8,128)(2,1)}), bf16[4,32,640]{2,1,0:T(8,128)(2,1)S(1)}, u32[]{:S(2)}, u32[]{:S(2)}) async-start(bf16[4,32,640]{2,1,0:T(8,128)(2,1)} %rows.1), calls=%async_computation | async-start | bytes 327680 | tf_op jit(solution)/shard_map/all_to_all | solution.py:342
  10.8 8.2 %collective-permute-start.2 = (bf16[64,256]{1,0:T(8,128)(2,1)}, bf16[64,256]{1,0:T(8,128)(2,1)S(1)}, u32[]{:S(2)}, u32[]{:S(2)}) collective-permute-start(bf16[64,256]{1,0:T(8,128)(2,1)} %param.12), channel_id=1, source_target_pairs={{0,256},{256,0},{1,257},{257,1},{2,258},{258,2},{3,259},{259,3},{4... | collective-permute-start | bytes 98312 | tf_op jit(solution)/shard_map/ppermute | solution.py:32
  19.1 4.8 %collective-permute-start.1 = (bf16[128,640]{1,0:T(8,128)(2,1)S(1)}, bf16[128,640]{1,0:T(8,128)(2,1)S(1)}, u32[]{:S(2)}, u32[]{:S(2)}) collective-permute-start(bf16[128,640]{1,0:T(8,128)(2,1)S(1)} %bitcast.19), channel_id=1, source_target_pairs={{0,10},{2,12},{4,14},{6,0},{8,2},{10,4},{12,6},{14,8},{1,11},{3,13... | collective-permute-start | bytes 491528 | tf_op jit(solution)/shard_map/ppermute | solution.py:32
  23.9 4.0 %collective-permute-start = (bf16[128,640]{1,0:T(8,128)(2,1)S(1)}, bf16[128,640]{1,0:T(8,128)(2,1)S(1)}, u32[]{:S(2)}, u32[]{:S(2)}) collective-permute-start(bf16[128,640]{1,0:T(8,128)(2,1)S(1)} %bitcast.20), channel_id=1, source_target_pairs={{0,6},{2,8},{4,10},{6,12},{8,14},{10,0},{12,2},{14,4},{1,7},{3,9},... | collective-permute-start | bytes 491528 | tf_op jit(solution)/shard_map/ppermute | solution.py:32
  28.0 0.8 pad_maximum_fusion.1
  28.7 0.7 broadcast_in_dim.13
  29.4 4.3 %all-to-all-start.1 = ((bf16[4,2,64,256]{3,2,1,0:T(8,128)(2,1)}), bf16[4,2,64,256]{3,2,1,0:T(8,128)(2,1)S(1)}, u32[]{:S(2)}, u32[]{:S(2)}) async-start(bf16[4,2,64,256]{3,2,1,0:T(8,128)(2,1)} %broadcast_in_dim.13), calls=%async_computation.1 | async-start | bytes 524288 | tf_op jit(solution)/shard_map/all_to_all | solution.py:37
  33.7 0.8 collective-permute-done.1
  34.5 3.0 %collective-permute-done = bf16[128,640]{1,0:T(8,128)(2,1)S(1)} collective-permute-done((bf16[128,640]{1,0:T(8,128)(2,1)S(1)}, bf16[128,640]{1,0:T(8,128)(2,1)S(1)}, u32[]{:S(2)}, u32[]{:S(2)}) %collective-permute-start) | collective-permute-done | bytes 163872 | tf_op jit(solution)/shard_map/ppermute | solution.py:32
  37.6 2.8 %all-to-all-done.1.pieces = bf16[4,2,64,256]{3,2,1,0:T(8,128)(2,1)S(1)} async-done(((bf16[4,2,64,256]{3,2,1,0:T(8,128)(2,1)}), bf16[4,2,64,256]{3,2,1,0:T(8,128)(2,1)S(1)}, u32[]{:S(2)}, u32[]{:S(2)}) %all-to-all-start.1) | async-done | bytes 262176 | tf_op jit(solution)/shard_map/all_to_all | solution.py:37
  40.5 4.2 %collective-permute-start.3 = (bf16[320,640]{1,0:T(8,128)(2,1)S(1)}, bf16[320,640]{1,0:T(8,128)(2,1)S(1)}, u32[]{:S(2)}, u32[]{:S(2)}) collective-permute-start(bf16[320,640]{1,0:T(8,128)(2,1)S(1)} %get-tuple-element.17), channel_id=1, source_target_pairs={{0,2},{2,4},{4,6},{6,8},{8,10},{10,12},{12,14},{14,0},{1,3},{3,5},... | collective-permute-start | bytes 1228808 | tf_op jit(solution)/shard_map/ppermute | solution.py:32
  44.7 1.9 %collective-permute-start.4 = (bf16[320,640]{1,0:T(8,128)(2,1)S(1)}, bf16[320,640]{1,0:T(8,128)(2,1)S(1)}, u32[]{:S(2)}, u32[]{:S(2)}) collective-permute-start(bf16[320,640]{1,0:T(8,128)(2,1)S(1)} %get-tuple-element.16), channel_id=1, source_target_pairs={{0,14},{2,0},{4,2},{6,4},{8,6},{10,8},{12,10},{14,12},{1,15},{3,1}... | collective-permute-start | bytes 1228808 | tf_op jit(solution)/shard_map/ppermute | solution.py:32
  46.6 7.0 %collective-permute-done.3 = bf16[320,640]{1,0:T(8,128)(2,1)S(1)} collective-permute-done((bf16[320,640]{1,0:T(8,128)(2,1)S(1)}, bf16[320,640]{1,0:T(8,128)(2,1)S(1)}, u32[]{:S(2)}, u32[]{:S(2)}) %collective-permute-start.3) | collective-permute-done | bytes 409632 | tf_op jit(solution)/shard_map/ppermute | solution.py:32
  53.6 5.3 %collective-permute-done.4 = bf16[320,640]{1,0:T(8,128)(2,1)S(1)} collective-permute-done((bf16[320,640]{1,0:T(8,128)(2,1)S(1)}, bf16[320,640]{1,0:T(8,128)(2,1)S(1)}, u32[]{:S(2)}, u32[]{:S(2)}) %collective-permute-start.4) | collective-permute-done | bytes 409632 | tf_op jit(solution)/shard_map/ppermute | solution.py:32
  59.0 1.9 %collective-permute-start.6 = (bf16[640,640]{1,0:T(8,128)(2,1)S(1)}, bf16[640,640]{1,0:T(8,128)(2,1)}, u32[]{:S(2)}, u32[]{:S(2)}) collective-permute-start(bf16[640,640]{1,0:T(8,128)(2,1)S(1)} %constant_dynamic-update-slice_fusion.far), channel_id=1, source_target_pairs={{0,1},{1,0},{2,3},{3,2},{4,5},{5,4},{6,7},{7,6},{8,9},{9,8},{10,11... | collective-permute-start | bytes 2457608 | tf_op jit(solution)/shard_map/ppermute | solution.py:32
  60.9 2.4 %collective-permute-start.5 = (bf16[384,640]{1,0:T(8,128)(2,1)S(1)}, bf16[384,640]{1,0:T(8,128)(2,1)}, u32[]{:S(2)}, u32[]{:S(2)}) collective-permute-start(bf16[384,640]{1,0:T(8,128)(2,1)S(1)} %pad_maximum_fusion.near), channel_id=1, source_target_pairs={{0,1},{1,0},{2,3},{3,2},{4,5},{5,4},{6,7},{7,6},{8,9},{9,8},{10,11... | collective-permute-start | bytes 1474568 | tf_op jit(solution)/shard_map/ppermute | solution.py:32
  64.1 0.8 collective-permute-done.5.near_other
  64.9 11.9 %head.1 = (bf16[2048,128]{1,0:T(8,128)(2,1)}, bf16[8,64,256]{2,1,0:T(8,128)(2,1)S(1)}) custom-call(s32[3]{0:T(128)S(1)} %pad_add_fusion.place, bf16[384,640]{1,0:T(8,128)(2,1)S(1)} %pad_maximum_fusion.near, bf16[640,640]{1,0:T(8,128)(2,1)S(1)} %constant_dynamic-update-slice_fusion.far, bf16[384,640]{1,0:T(8,128)(2,1)} %collective-permute-done.5.near_other, ...), custom_call_target="tpu_custom_call" | custom-call | flops 3000000000 | bytes 8000000 | tf_op jit(solution)/shard_map/head/pallas_call | solution.py:308
  76.8 17.8 %all_to_all.15 = bf16[8,64,256]{2,1,0:T(8,128)(2,1)S(1)} all-to-all(bf16[8,64,256]{2,1,0:T(8,128)(2,1)S(1)} %get-tuple-element.15), channel_id=1, replica_groups=mesh['zh'=2,'x'=4,'zl'=4,'y'=8,'c'=2] {'zh','x'}, dimensions={0} | all-to-all | bytes 524288 | tf_op jit(solution)/shard_map/all_to_all | solution.py:356
  94.5 0.7 fusion
  (20 shorter events, 0.9 us)
Async XLA Ops:
  0.6 0.8 copy-start.3
  1.4 0.7 copy-start.4
  2.1 0.7 copy-start.5
  3.6 15.5 %all-to-all-start = ((bf16[4,32,640]{2,1,0:T(8,128)(2,1)}), bf16[4,32,640]{2,1,0:T(8,128)(2,1)S(1)}, u32[]{:S(2)}, u32[]{:S(2)}) async-start(bf16[4,32,640]{2,1,0:T(8,128)(2,1)} %rows.1), calls=%async_computation | async-start | bytes 327680 | tf_op jit(solution)/shard_map/all_to_all | solution.py:342
  10.8 17.1 %collective-permute-start.2 = (bf16[64,256]{1,0:T(8,128)(2,1)}, bf16[64,256]{1,0:T(8,128)(2,1)S(1)}, u32[]{:S(2)}, u32[]{:S(2)}) collective-permute-start(bf16[64,256]{1,0:T(8,128)(2,1)} %param.12), channel_id=1, source_target_pairs={{0,256},{256,0},{1,257},{257,1},{2,258},{258,2},{3,259},{259,3},{4... | collective-permute-start | bytes 98312 | tf_op jit(solution)/shard_map/ppermute | solution.py:32
  19.1 15.5 %collective-permute-start.1 = (bf16[128,640]{1,0:T(8,128)(2,1)S(1)}, bf16[128,640]{1,0:T(8,128)(2,1)S(1)}, u32[]{:S(2)}, u32[]{:S(2)}) collective-permute-start(bf16[128,640]{1,0:T(8,128)(2,1)S(1)} %bitcast.19), channel_id=1, source_target_pairs={{0,10},{2,12},{4,14},{6,0},{8,2},{10,4},{12,6},{14,8},{1,11},{3,13... | collective-permute-start | bytes 491528 | tf_op jit(solution)/shard_map/ppermute | solution.py:32
  23.9 13.6 %collective-permute-start = (bf16[128,640]{1,0:T(8,128)(2,1)S(1)}, bf16[128,640]{1,0:T(8,128)(2,1)S(1)}, u32[]{:S(2)}, u32[]{:S(2)}) collective-permute-start(bf16[128,640]{1,0:T(8,128)(2,1)S(1)} %bitcast.20), channel_id=1, source_target_pairs={{0,6},{2,8},{4,10},{6,12},{8,14},{10,0},{12,2},{14,4},{1,7},{3,9},... | collective-permute-start | bytes 491528 | tf_op jit(solution)/shard_map/ppermute | solution.py:32
  29.4 11.0 %all-to-all-start.1 = ((bf16[4,2,64,256]{3,2,1,0:T(8,128)(2,1)}), bf16[4,2,64,256]{3,2,1,0:T(8,128)(2,1)S(1)}, u32[]{:S(2)}, u32[]{:S(2)}) async-start(bf16[4,2,64,256]{3,2,1,0:T(8,128)(2,1)} %broadcast_in_dim.13), calls=%async_computation.1 | async-start | bytes 524288 | tf_op jit(solution)/shard_map/all_to_all | solution.py:37
  37.6 25.7 %copy-start = (bf16[1,2048,192]{1,2,0:T(8,128)(2,1)S(1)}, bf16[1,2048,192]{1,2,0:T(8,128)(2,1)}, u32[]{:S(2)}) copy-start(bf16[1,2048,192]{1,2,0:T(8,128)(2,1)} %param.8) | copy-start | bytes 2359300
  37.6 25.7 %copy-start.1 = (bf16[1,2048,128]{2,1,0:T(8,128)(2,1)S(1)}, bf16[1,2048,128]{2,1,0:T(8,128)(2,1)}, u32[]{:S(2)}) copy-start(bf16[1,2048,128]{2,1,0:T(8,128)(2,1)} %param.13) | copy-start | bytes 1572868
  37.6 25.7 %copy-start.2 = (f32[264,256]{1,0:T(8,128)S(1)}, f32[264,256]{1,0:T(8,128)}, u32[]{:S(2)}) copy-start(f32[264,256]{1,0:T(8,128)} %constant.18.clone.table_in) | copy-start | bytes 811012
  40.5 13.1 %collective-permute-start.3 = (bf16[320,640]{1,0:T(8,128)(2,1)S(1)}, bf16[320,640]{1,0:T(8,128)(2,1)S(1)}, u32[]{:S(2)}, u32[]{:S(2)}) collective-permute-start(bf16[320,640]{1,0:T(8,128)(2,1)S(1)} %get-tuple-element.17), channel_id=1, source_target_pairs={{0,2},{2,4},{4,6},{6,8},{8,10},{10,12},{12,14},{14,0},{1,3},{3,5},... | collective-permute-start | bytes 1228808 | tf_op jit(solution)/shard_map/ppermute | solution.py:32
  44.7 14.2 %collective-permute-start.4 = (bf16[320,640]{1,0:T(8,128)(2,1)S(1)}, bf16[320,640]{1,0:T(8,128)(2,1)S(1)}, u32[]{:S(2)}, u32[]{:S(2)}) collective-permute-start(bf16[320,640]{1,0:T(8,128)(2,1)S(1)} %get-tuple-element.16), channel_id=1, source_target_pairs={{0,14},{2,0},{4,2},{6,4},{8,6},{10,8},{12,10},{14,12},{1,15},{3,1}... | collective-permute-start | bytes 1228808 | tf_op jit(solution)/shard_map/ppermute | solution.py:32
  59.0 5.9 %collective-permute-start.6 = (bf16[640,640]{1,0:T(8,128)(2,1)S(1)}, bf16[640,640]{1,0:T(8,128)(2,1)}, u32[]{:S(2)}, u32[]{:S(2)}) collective-permute-start(bf16[640,640]{1,0:T(8,128)(2,1)S(1)} %constant_dynamic-update-slice_fusion.far), channel_id=1, source_target_pairs={{0,1},{1,0},{2,3},{3,2},{4,5},{5,4},{6,7},{7,6},{8,9},{9,8},{10,11... | collective-permute-start | bytes 2457608 | tf_op jit(solution)/shard_map/ppermute | solution.py:32
  60.9 4.0 %collective-permute-start.5 = (bf16[384,640]{1,0:T(8,128)(2,1)S(1)}, bf16[384,640]{1,0:T(8,128)(2,1)}, u32[]{:S(2)}, u32[]{:S(2)}) collective-permute-start(bf16[384,640]{1,0:T(8,128)(2,1)S(1)} %pad_maximum_fusion.near), channel_id=1, source_target_pairs={{0,1},{1,0},{2,3},{3,2},{4,5},{5,4},{6,7},{7,6},{8,9},{9,8},{10,11... | collective-permute-start | bytes 1474568 | tf_op jit(solution)/shard_map/ppermute | solution.py:32
  64.9 29.6 %copy-start.6 = (f32[64,256]{1,0:T(8,128)S(1)}, f32[64,256]{1,0:T(8,128)}, u32[]{:S(2)}) copy-start(f32[64,256]{1,0:T(8,128)} %param.14) | copy-start | bytes 196612

commit v3 on v2

--- a/solution.py
+++ b/solution.py
@@ -15,6 +15,7 @@
 D_VAL = 128
 D_ROW = 640
 BLOCK = 256
+HEAD_VMEM = 50 * 1024 * 1024
 SEQ = ("zl", "y", "c")
 DP = ("zh", "x")
 
@@ -75,7 +76,7 @@
             pltpu.VMEM(segments.shape, jnp.int32),
             pltpu.SemaphoreType.DMA((3,)),
         ],
-        compiler_params=pltpu.CompilerParams(vmem_limit_bytes=4 * 1024 * 1024),
+        compiler_params=pltpu.CompilerParams(vmem_limit_bytes=60 * 1024 * 1024),
         name="rows",
     )(latent, latent_gain[None], segments)
 
@@ -161,14 +162,22 @@
 
 
 def kernel(
-    place, near, far, near_other, far_other, query_parts, grads, table, pieces,
+    place, near, far, near_other_in, far_other, query_parts_in, grads_in, table_in, pieces,
     out, gradient,
-    result_rows,
+    near_other, query_parts, grads, table, arrived, result_rows,
     weight, lat, hot, key, query, val, val_t, starts, key_grad, val_grad, firsts, left,
 ):
     length = lat.shape[0]
     blocks = length // BLOCK
     y, c = place[0], place[1]
+    copies = [
+        pltpu.make_async_copy(source, target, arrived.at[i])
+        for i, (source, target) in enumerate(
+            ((near_other_in, near_other), (table_in, table), (query_parts_in, query_parts), (grads_in, grads))
+        )
+    ]
+    for copy in copies:
+        copy.start()
     own = near.shape[0] // len(NEAR)
 
     def put(source, held, core):
@@ -179,6 +188,7 @@
     put(near, NEAR, c)
     put(far, FAR, c)
     put(far_other, FAR, 1 - c)
+    copies[0].wait()
     put(near_other, NEAR, 1 - c)
     share = pieces.shape[2]
     for x in range(4):
@@ -203,13 +213,16 @@
     lane8 = lax.broadcasted_iota(jnp.int32, (8, 128), 1)
     row8 = lax.broadcasted_iota(jnp.int32, (8, 128), 0)
     first8 = jnp.broadcast_to(first, (8, 128))
+    copies[1].wait()
     column = jnp.sum(jnp.where(lane8 == row8, first8, 0).astype(f32), axis=1, keepdims=True)
     low = first8 & 255
     split = jnp.where(lane8 < 8, first8 - low, jnp.where(lane8 < 16, low, 0))
     split = split.astype(f32).astype(bf16)
 
 
-    @pl.loop(0, blocks, unroll=2)
+    copies[2].wait()
+
+    @pl.loop(0, blocks, unroll=4)
     def prepare(i):
         at = pl.multiple_of(i * BLOCK, BLOCK)
         rows = pl.ds(at, BLOCK)
@@ -240,6 +253,7 @@
         key_grad[rows, :] = jnp.zeros((BLOCK, D_NOPE), f32)
         val_grad[rows, :] = jnp.zeros((BLOCK, D_VAL), f32)
 
+    copies[3].wait()
     token = lax.broadcasted_iota(jnp.int32, (BLOCK, BLOCK), 0)
     asker = lax.broadcasted_iota(jnp.int32, (BLOCK, BLOCK), 1)
 
@@ -305,15 +319,21 @@
 def head(place, near, far, near_other, far_other, query_parts, grads, table, pieces):
     length = grads.shape[0]
     vmem = pl.BlockSpec(memory_space=pltpu.VMEM)
+    hbm = pl.BlockSpec(memory_space=pltpu.HBM)
     return pl.pallas_call(
         kernel,
         out_shape=(
             jax.ShapeDtypeStruct((length, D_VAL), bf16),
             jax.ShapeDtypeStruct((8, D_LAT // 8, D_NOPE + D_VAL), bf16),
         ),
-        in_specs=[pl.BlockSpec(memory_space=pltpu.SMEM)] + [vmem] * 8,
+        in_specs=[pl.BlockSpec(memory_space=pltpu.SMEM)] + [vmem, vmem, hbm, vmem, hbm, hbm, hbm, vmem],
         out_specs=(pl.BlockSpec(memory_space=pltpu.HBM), vmem),
         scratch_shapes=[
+            pltpu.VMEM(near_other.shape, bf16),
+            pltpu.VMEM(query_parts.shape, bf16),
+            pltpu.VMEM(grads.shape, bf16),
+            pltpu.VMEM(table.shape, f32),
+            pltpu.SemaphoreType.DMA((4,)),
             pltpu.VMEM((length, D_VAL), bf16),
             pltpu.VMEM((D_LAT, D_NOPE + D_VAL), bf16),
             pltpu.VMEM((length, D_ROW), bf16),
@@ -328,7 +348,7 @@
             pltpu.SMEM((length // BLOCK,), jnp.int32),
             pltpu.SemaphoreType.DMA((length // BLOCK,)),
         ],
-        compiler_params=pltpu.CompilerParams(vmem_limit_bytes=18 * 1024 * 1024),
+        compiler_params=pltpu.CompilerParams(vmem_limit_bytes=HEAD_VMEM),
         cost_estimate=pl.CostEstimate(flops=3_000_000_000, bytes_accessed=8_000_000, transcendentals=2_000_000),
         name="head",
     )(place, near, far, near_other, far_other, query_parts, grads, table, pieces)

time: 95.9 us -> 95 us (level)
  Pallas kernels: 13.3 us -> 14.4 us
    unnamed x15 -> x11, local copies, waits for them, and re-layouts: 2.17 us -> 1.22 us
  transfers between devices with their start and end apart: 9 -> 9, of which waited for: 6 -> 5; matrix products, arithmetic and copies ran while one was open for 2% -> 2% of each run, Pallas kernels for 1% -> 1%
where the time goes in v3:
time: 95 us; the launch traced here: 94.3 us
  starting transfers between devices  39.1 us (41%)
  waiting for transfers between devices  18.8 us (20%)
  blocking collectives  17.6 us (19%)
  Pallas kernels  14.4 us (15%)
  local copies, waits for them, and re-layouts  2.06 us (2%)
  other arithmetic  1.57 us (2%)
    ppermute x7, starting transfers between devices, shifted(): return lax.ppermute(x, axis, [(i, (i + step) % size) for i in range(size)])  27.5 us
    all_to_all x1, blocking collectives, local(): parts = lax.all_to_all(grad, DP, 0, 0, tiled=True)  17.6 us
    ppermute x7, waiting for transfers between devices, shifted(): return lax.ppermute(x, axis, [(i, (i + step) % size) for i in range(size)])  16.1 us
    pallas_call x1, Pallas kernels, head(): pl.pallas_call(kernel, out_shape=(jax.ShapeDtypeStruct((length, D_VAL), b...  12.2 us
    all_to_all x1, starting transfers between devices, local(): line = lax.all_to_all(sent, 'zl', 0, 0, tiled=True).reshape(-1, D_ROW)  7.27 us
    all_to_all x1, starting transfers between devices, copy_for_each(): lax.all_to_all(jnp.broadcast_to(x[None], (size, *x.shape)), axis, 0, 0, t...  4.29 us
    all_to_all x1, waiting for transfers between devices, copy_for_each(): lax.all_to_all(jnp.broadcast_to(x[None], (size, *x.shape)), axis, 0, 0, t...  2.78 us
  transfers between devices with their start and end apart: 9, of which 5 were waited for; matrix products, arithmetic and copies ran while one was open for 2% of the time, Pallas kernels for 1%

profile of v3, /device:TPU:56, one launch (start us, length us, event | category | flops | bytes accessed | tf_op | source)
XLA Modules:
  0.0 94.3 jit_solution(7930585163692938699)
XLA Ops:
  0.6 1.6 %rows.1 = bf16[4,32,640]{2,1,0:T(8,128)(2,1)} custom-call(bf16[32,576]{1,0:T(8,128)(2,1)} %bitcast.20, f32[1,512]{1,0:T(1,128)} %bitcast.23, s32[1,32]{1,0:T(1,128)} %numbers_in.1), custom_call_target="tpu_custom_call" | custom-call | tf_op jit(solution)/shard_map/rows/pallas_call | solution.py:68
  2.2 7.3 %all-to-all-start = ((bf16[4,32,640]{2,1,0:T(8,128)(2,1)}), bf16[4,32,640]{2,1,0:T(8,128)(2,1)S(1)}, u32[]{:S(2)}, u32[]{:S(2)}) async-start(bf16[4,32,640]{2,1,0:T(8,128)(2,1)} %rows.1), calls=%async_computation | async-start | bytes 327680 | tf_op jit(solution)/shard_map/all_to_all | solution.py:362
  9.5 8.2 %collective-permute-start.2 = (bf16[64,256]{1,0:T(8,128)(2,1)}, bf16[64,256]{1,0:T(8,128)(2,1)S(1)}, u32[]{:S(2)}, u32[]{:S(2)}) collective-permute-start(bf16[64,256]{1,0:T(8,128)(2,1)} %param.12), channel_id=1, source_target_pairs={{0,256},{256,0},{1,257},{257,1},{2,258},{258,2},{3,259},{259,3},{4... | collective-permute-start | bytes 98312 | tf_op jit(solution)/shard_map/ppermute | solution.py:33
  17.7 4.8 %collective-permute-start.1 = (bf16[128,640]{1,0:T(8,128)(2,1)S(1)}, bf16[128,640]{1,0:T(8,128)(2,1)S(1)}, u32[]{:S(2)}, u32[]{:S(2)}) collective-permute-start(bf16[128,640]{1,0:T(8,128)(2,1)S(1)} %bitcast.17), channel_id=1, source_target_pairs={{0,10},{2,12},{4,14},{6,0},{8,2},{10,4},{12,6},{14,8},{1,11},{3,13... | collective-permute-start | bytes 491528 | tf_op jit(solution)/shard_map/ppermute | solution.py:33
  22.5 4.0 %collective-permute-start = (bf16[128,640]{1,0:T(8,128)(2,1)S(1)}, bf16[128,640]{1,0:T(8,128)(2,1)S(1)}, u32[]{:S(2)}, u32[]{:S(2)}) collective-permute-start(bf16[128,640]{1,0:T(8,128)(2,1)S(1)} %bitcast.18), channel_id=1, source_target_pairs={{0,6},{2,8},{4,10},{6,12},{8,14},{10,0},{12,2},{14,4},{1,7},{3,9},... | collective-permute-start | bytes 491528 | tf_op jit(solution)/shard_map/ppermute | solution.py:33
  26.6 0.8 pad_maximum_fusion.1
  27.4 0.7 broadcast_in_dim.13
  28.1 4.3 %all-to-all-start.1 = ((bf16[4,2,64,256]{3,2,1,0:T(8,128)(2,1)}), bf16[4,2,64,256]{3,2,1,0:T(8,128)(2,1)S(1)}, u32[]{:S(2)}, u32[]{:S(2)}) async-start(bf16[4,2,64,256]{3,2,1,0:T(8,128)(2,1)} %broadcast_in_dim.13), calls=%async_computation.1 | async-start | bytes 524288 | tf_op jit(solution)/shard_map/all_to_all | solution.py:38
  32.4 0.8 collective-permute-done.1
  33.2 3.0 %collective-permute-done = bf16[128,640]{1,0:T(8,128)(2,1)S(1)} collective-permute-done((bf16[128,640]{1,0:T(8,128)(2,1)S(1)}, bf16[128,640]{1,0:T(8,128)(2,1)S(1)}, u32[]{:S(2)}, u32[]{:S(2)}) %collective-permute-start) | collective-permute-done | bytes 163872 | tf_op jit(solution)/shard_map/ppermute | solution.py:33
  36.3 2.8 %all-to-all-done.1.pieces = bf16[4,2,64,256]{3,2,1,0:T(8,128)(2,1)S(1)} async-done(((bf16[4,2,64,256]{3,2,1,0:T(8,128)(2,1)}), bf16[4,2,64,256]{3,2,1,0:T(8,128)(2,1)S(1)}, u32[]{:S(2)}, u32[]{:S(2)}) %all-to-all-start.1) | async-done | bytes 262176 | tf_op jit(solution)/shard_map/all_to_all | solution.py:38
  39.1 0.1 fusion.1
  39.1 4.2 %collective-permute-start.3 = (bf16[320,640]{1,0:T(8,128)(2,1)S(1)}, bf16[320,640]{1,0:T(8,128)(2,1)S(1)}, u32[]{:S(2)}, u32[]{:S(2)}) collective-permute-start(bf16[320,640]{1,0:T(8,128)(2,1)S(1)} %get-tuple-element.17), channel_id=1, source_target_pairs={{0,2},{2,4},{4,6},{6,8},{8,10},{10,12},{12,14},{14,0},{1,3},{3,5},... | collective-permute-start | bytes 1228808 | tf_op jit(solution)/shard_map/ppermute | solution.py:33
  43.3 1.9 %collective-permute-start.4 = (bf16[320,640]{1,0:T(8,128)(2,1)S(1)}, bf16[320,640]{1,0:T(8,128)(2,1)S(1)}, u32[]{:S(2)}, u32[]{:S(2)}) collective-permute-start(bf16[320,640]{1,0:T(8,128)(2,1)S(1)} %get-tuple-element.16), channel_id=1, source_target_pairs={{0,14},{2,0},{4,2},{6,4},{8,6},{10,8},{12,10},{14,12},{1,15},{3,1}... | collective-permute-start | bytes 1228808 | tf_op jit(solution)/shard_map/ppermute | solution.py:33
  45.3 7.0 %collective-permute-done.3 = bf16[320,640]{1,0:T(8,128)(2,1)S(1)} collective-permute-done((bf16[320,640]{1,0:T(8,128)(2,1)S(1)}, bf16[320,640]{1,0:T(8,128)(2,1)S(1)}, u32[]{:S(2)}, u32[]{:S(2)}) %collective-permute-start.3) | collective-permute-done | bytes 409632 | tf_op jit(solution)/shard_map/ppermute | solution.py:33
  52.2 5.3 %collective-permute-done.4 = bf16[320,640]{1,0:T(8,128)(2,1)S(1)} collective-permute-done((bf16[320,640]{1,0:T(8,128)(2,1)S(1)}, bf16[320,640]{1,0:T(8,128)(2,1)S(1)}, u32[]{:S(2)}, u32[]{:S(2)}) %collective-permute-start.4) | collective-permute-done | bytes 409632 | tf_op jit(solution)/shard_map/ppermute | solution.py:33
  57.6 1.9 %collective-permute-start.6 = (bf16[640,640]{1,0:T(8,128)(2,1)S(1)}, bf16[640,640]{1,0:T(8,128)(2,1)}, u32[]{:S(2)}, u32[]{:S(2)}) collective-permute-start(bf16[640,640]{1,0:T(8,128)(2,1)S(1)} %constant_dynamic-update-slice_fusion.far), channel_id=1, source_target_pairs={{0,1},{1,0},{2,3},{3,2},{4,5},{5,4},{6,7},{7,6},{8,9},{9,8},{10,11... | collective-permute-start | bytes 2457608 | tf_op jit(solution)/shard_map/ppermute | solution.py:33
  59.5 2.4 %collective-permute-start.5 = (bf16[384,640]{1,0:T(8,128)(2,1)S(1)}, bf16[384,640]{1,0:T(8,128)(2,1)}, u32[]{:S(2)}, u32[]{:S(2)}) collective-permute-start(bf16[384,640]{1,0:T(8,128)(2,1)S(1)} %pad_maximum_fusion.near), channel_id=1, source_target_pairs={{0,1},{1,0},{2,3},{3,2},{4,5},{5,4},{6,7},{7,6},{8,9},{9,8},{10,11... | collective-permute-start | bytes 1474568 | tf_op jit(solution)/shard_map/ppermute | solution.py:33
  62.0 0.6 stage.1
  62.6 1.2 %copy-done.3 = bf16[2048,384]{1,0:T(8,128)(2,1)} copy-done((bf16[2048,384]{1,0:T(8,128)(2,1)}, bf16[2048,384]{1,0:T(8,128)(2,1)S(1)}, u32[]{:S(2)}) %copy-start.3) | copy-done | bytes 1572888
  63.8 0.1 pad_add_fusion.place
  63.9 12.2 %head.1 = (bf16[2048,128]{1,0:T(8,128)(2,1)}, bf16[8,64,256]{2,1,0:T(8,128)(2,1)S(1)}) custom-call(s32[3]{0:T(128)S(1)} %pad_add_fusion.place, bf16[384,640]{1,0:T(8,128)(2,1)S(1)} %pad_maximum_fusion.near, bf16[640,640]{1,0:T(8,128)(2,1)S(1)} %constant_dynamic-update-slice_fusion.far, bf16[384,640]{1,0:T(8,128)(2,1)} %collective-permute-done.5.near_other_in, ...), custom_call_target="tpu_custom_call" | custom-call | flops 3000000000 | bytes 8000000 | tf_op jit(solution)/shard_map/head/pallas_call | solution.py:323
  76.1 17.6 %all_to_all.15 = bf16[8,64,256]{2,1,0:T(8,128)(2,1)S(1)} all-to-all(bf16[8,64,256]{2,1,0:T(8,128)(2,1)S(1)} %get-tuple-element.15), channel_id=1, replica_groups=mesh['zh'=2,'x'=4,'zl'=4,'y'=8,'c'=2] {'zh','x'}, dimensions={0} | all-to-all | bytes 524288 | tf_op jit(solution)/shard_map/all_to_all | solution.py:376
  93.6 0.7 fusion
  (16 shorter events, 0.2 us)
Async XLA Ops:
  2.2 15.5 %all-to-all-start = ((bf16[4,32,640]{2,1,0:T(8,128)(2,1)}), bf16[4,32,640]{2,1,0:T(8,128)(2,1)S(1)}, u32[]{:S(2)}, u32[]{:S(2)}) async-start(bf16[4,32,640]{2,1,0:T(8,128)(2,1)} %rows.1), calls=%async_computation | async-start | bytes 327680 | tf_op jit(solution)/shard_map/all_to_all | solution.py:362
  9.5 17.1 %collective-permute-start.2 = (bf16[64,256]{1,0:T(8,128)(2,1)}, bf16[64,256]{1,0:T(8,128)(2,1)S(1)}, u32[]{:S(2)}, u32[]{:S(2)}) collective-permute-start(bf16[64,256]{1,0:T(8,128)(2,1)} %param.12), channel_id=1, source_target_pairs={{0,256},{256,0},{1,257},{257,1},{2,258},{258,2},{3,259},{259,3},{4... | collective-permute-start | bytes 98312 | tf_op jit(solution)/shard_map/ppermute | solution.py:33
  17.7 15.5 %collective-permute-start.1 = (bf16[128,640]{1,0:T(8,128)(2,1)S(1)}, bf16[128,640]{1,0:T(8,128)(2,1)S(1)}, u32[]{:S(2)}, u32[]{:S(2)}) collective-permute-start(bf16[128,640]{1,0:T(8,128)(2,1)S(1)} %bitcast.17), channel_id=1, source_target_pairs={{0,10},{2,12},{4,14},{6,0},{8,2},{10,4},{12,6},{14,8},{1,11},{3,13... | collective-permute-start | bytes 491528 | tf_op jit(solution)/shard_map/ppermute | solution.py:33
  22.5 13.6 %collective-permute-start = (bf16[128,640]{1,0:T(8,128)(2,1)S(1)}, bf16[128,640]{1,0:T(8,128)(2,1)S(1)}, u32[]{:S(2)}, u32[]{:S(2)}) collective-permute-start(bf16[128,640]{1,0:T(8,128)(2,1)S(1)} %bitcast.18), channel_id=1, source_target_pairs={{0,6},{2,8},{4,10},{6,12},{8,14},{10,0},{12,2},{14,4},{1,7},{3,9},... | collective-permute-start | bytes 491528 | tf_op jit(solution)/shard_map/ppermute | solution.py:33
  28.1 11.0 %all-to-all-start.1 = ((bf16[4,2,64,256]{3,2,1,0:T(8,128)(2,1)}), bf16[4,2,64,256]{3,2,1,0:T(8,128)(2,1)S(1)}, u32[]{:S(2)}, u32[]{:S(2)}) async-start(bf16[4,2,64,256]{3,2,1,0:T(8,128)(2,1)} %broadcast_in_dim.13), calls=%async_computation.1 | async-start | bytes 524288 | tf_op jit(solution)/shard_map/all_to_all | solution.py:38
  36.2 25.7 %copy-start = (bf16[1,2048,192]{1,2,0:T(8,128)(2,1)S(1)}, bf16[1,2048,192]{1,2,0:T(8,128)(2,1)}, u32[]{:S(2)}) copy-start(bf16[1,2048,192]{1,2,0:T(8,128)(2,1)} %param.8) | copy-start | bytes 2359300
  36.2 25.7 %copy-start.1 = (bf16[1,2048,128]{2,1,0:T(8,128)(2,1)S(1)}, bf16[1,2048,128]{2,1,0:T(8,128)(2,1)}, u32[]{:S(2)}) copy-start(bf16[1,2048,128]{2,1,0:T(8,128)(2,1)} %param.13) | copy-start | bytes 1572868
  36.3 25.7 %copy-start.2 = (f32[264,256]{1,0:T(8,128)S(1)}, f32[264,256]{1,0:T(8,128)}, u32[]{:S(2)}) copy-start(f32[264,256]{1,0:T(8,128)} %constant.18.clone.table_in) | copy-start | bytes 811012
  39.1 13.1 %collective-permute-start.3 = (bf16[320,640]{1,0:T(8,128)(2,1)S(1)}, bf16[320,640]{1,0:T(8,128)(2,1)S(1)}, u32[]{:S(2)}, u32[]{:S(2)}) collective-permute-start(bf16[320,640]{1,0:T(8,128)(2,1)S(1)} %get-tuple-element.17), channel_id=1, source_target_pairs={{0,2},{2,4},{4,6},{6,8},{8,10},{10,12},{12,14},{14,0},{1,3},{3,5},... | collective-permute-start | bytes 1228808 | tf_op jit(solution)/shard_map/ppermute | solution.py:33
  43.3 14.2 %collective-permute-start.4 = (bf16[320,640]{1,0:T(8,128)(2,1)S(1)}, bf16[320,640]{1,0:T(8,128)(2,1)S(1)}, u32[]{:S(2)}, u32[]{:S(2)}) collective-permute-start(bf16[320,640]{1,0:T(8,128)(2,1)S(1)} %get-tuple-element.16), channel_id=1, source_target_pairs={{0,14},{2,0},{4,2},{6,4},{8,6},{10,8},{12,10},{14,12},{1,15},{3,1}... | collective-permute-start | bytes 1228808 | tf_op jit(solution)/shard_map/ppermute | solution.py:33
  57.6 6.3 %collective-permute-start.6 = (bf16[640,640]{1,0:T(8,128)(2,1)S(1)}, bf16[640,640]{1,0:T(8,128)(2,1)}, u32[]{:S(2)}, u32[]{:S(2)}) collective-permute-start(bf16[640,640]{1,0:T(8,128)(2,1)S(1)} %constant_dynamic-update-slice_fusion.far), channel_id=1, source_target_pairs={{0,1},{1,0},{2,3},{3,2},{4,5},{5,4},{6,7},{7,6},{8,9},{9,8},{10,11... | collective-permute-start | bytes 2457608 | tf_op jit(solution)/shard_map/ppermute | solution.py:33
  59.5 4.3 %collective-permute-start.5 = (bf16[384,640]{1,0:T(8,128)(2,1)S(1)}, bf16[384,640]{1,0:T(8,128)(2,1)}, u32[]{:S(2)}, u32[]{:S(2)}) collective-permute-start(bf16[384,640]{1,0:T(8,128)(2,1)S(1)} %pad_maximum_fusion.near), channel_id=1, source_target_pairs={{0,1},{1,0},{2,3},{3,2},{4,5},{5,4},{6,7},{7,6},{8,9},{9,8},{10,11... | collective-permute-start | bytes 1474568 | tf_op jit(solution)/shard_map/ppermute | solution.py:33
  62.6 1.2 %copy-start.3 = (bf16[2048,384]{1,0:T(8,128)(2,1)}, bf16[2048,384]{1,0:T(8,128)(2,1)S(1)}, u32[]{:S(2)}) copy-start(bf16[2048,384]{1,0:T(8,128)(2,1)S(1)} %get-tuple-element.10.query_parts_in) | copy-start | bytes 4718596
  63.9 29.8 %copy-start.4 = (f32[64,256]{1,0:T(8,128)S(1)}, f32[64,256]{1,0:T(8,128)}, u32[]{:S(2)}) copy-start(f32[64,256]{1,0:T(8,128)} %param.14) | copy-start | bytes 196612
